TPU v7x, 32 devices: a whole 2x2x4 slice. The times are simulated.
32 devices in a mesh: ep: 4 (over y, core), fs: 8 (over z, x).
Axes of the slice: x: 2, y: 2, z: 4, core: 2. Of those that a mesh axis runs over, the one named last changes fastest.
Arguments:
- grads: bfloat16 [4, 4, 128, 14336], P('ep', None, 'fs'), may hold values from -64 to 64
- counts: int32 [4, 4], replicated, may hold values from 16 to 2047
- weight: bfloat16 [4, 128, 14336], P('ep', 'fs'), may hold values from -3 to 3
- mom: float32 [4, 128, 14336], P('ep', 'fs'), may hold values from -64 to 64
- second: float32 [4, 128, 14336], P('ep', 'fs'), may hold values from 0.1 to 10
- in_weight: float32 [6, 32], replicated, may hold values from -2.5 to 2.5
- in_bias: float32 [32], replicated, may hold values from -3 to 3
- out_weight: float32 [32, 2], replicated, may hold values from -1 to 1
- out_bias: float32 [2], replicated, may hold values from -3 to 3
Outputs:
- new_weight: bfloat16 [4, 128, 14336], P('ep')
- new_mom: float32 [4, 128, 14336], P('ep', 'fs')
- new_second: float32 [4, 128, 14336], P('ep', 'fs')
All inputs are finite; a program needn't handle non-finite values.
Results may differ from a plain program's by a relative error of at most 0.0019.
Values may be sent and summed in bfloat16 or wider, within the bound.
A program may use at most 64 MiB of HBM per device.

v0:
```python
import functools

import jax
import jax.numpy as jnp
from jax import lax
from jax.experimental import pallas as pl
from jax.experimental.pallas import tpu as pltpu
from jax.sharding import PartitionSpec as P

MOMENTUM_DECAY = 0.9
SECOND_DECAY = 0.99
NORM_EPS = 1e-06
ROOT_EPS = 1e-08
STEP_SCALE = 0.2
EXP_SCALE = 0.5
LANES = 128
MOST_CHUNKS = 14
MOST_CUTS = 4
LAG = 3
VMEM_BYTES = 67043328


def largest_divisor(number, most):
    return max(d for d in range(1, most + 1) if number % d == 0)


def tile_width(columns, most):
    return LANES * largest_divisor(columns // LANES, most // LANES)


def turned_chunks(depth, across, chunks):
    def load(turned):
        straight = chunks - turned
        on_x = (across - 1) * (depth * straight + turned)
        on_z = (depth - 1) * (straight + across * turned)
        return max(on_x, on_z)

    return min(range(chunks + 1), key=load)


def remote(src, dst, send_sem, recv_sem, axis, peer):
    return pltpu.make_async_remote_copy(
        src_ref=src,
        dst_ref=dst,
        send_sem=send_sem,
        recv_sem=recv_sem,
        device_id={axis: peer},
        device_id_type=pl.DeviceIdType.MESH,
    )


def kernel(
    groups,
    depth,
    across,
    chunks,
    counts_hbm,
    in_weight_hbm,
    in_bias_hbm,
    out_weight_hbm,
    out_bias_hbm,
    grads_hbm,
    weight_hbm,
    mom_hbm,
    second_hbm,
    gathered_hbm,
    mom_hbm_out,
    second_hbm_out,
    counts,
    in_weight,
    in_bias,
    out_weight,
    out_bias,
    grads,
    weight,
    mom,
    second,
    gathered,
    outgoing,
    arrived,
    gradient,
    sums,
    bias,
    small_sem,
    slab_sem,
    param_sem,
    grad_send,
    grad_recv,
    flush_sem,
    state_sem,
    sum_send,
    sum_recv,
    row_send,
    row_recv,
):
    shards = depth * across
    rows, columns = mom.shape
    units = in_bias.shape[0]
    me_group = lax.axis_index("ep")
    me = lax.axis_index("fs")
    z = me // across
    x = me % across

    def peer_of(step):
        return (me_group + step) % groups

    small = [
        pltpu.make_async_copy(src, dst, small_sem.at[i])
        for i, (src, dst) in enumerate(
            (
                (counts_hbm, counts),
                (in_weight_hbm, in_weight),
                (in_bias_hbm, in_bias),
                (out_weight_hbm, out_weight),
                (out_bias_hbm, out_bias),
            )
        )
    ]
    for copy in small:
        copy.start()

    slabs = [
        pltpu.make_async_copy(
            grads_hbm.at[0, peer_of(step)], grads.at[step], slab_sem.at[step]
        )
        for step in range(groups)
    ]
    for copy in slabs[1:] + slabs[:1]:
        copy.start()
    params = [
        pltpu.make_async_copy(src.at[0], dst, param_sem.at[i])
        for i, (src, dst) in enumerate(
            (
                (mom_hbm, mom),
                (second_hbm, second),
                (weight_hbm, weight),
            )
        )
    ]
    for copy in params:
        copy.start()

    barrier = pltpu.get_barrier_semaphore()
    for step in range(1, groups):
        pl.semaphore_signal(
            barrier,
            inc=1,
            device_id={"ep": peer_of(step)},
            device_id_type=pl.DeviceIdType.MESH,
        )
    for step in range(1, shards):
        pl.semaphore_signal(
            barrier,
            inc=1,
            device_id={"fs": (me + step) % shards},
            device_id_type=pl.DeviceIdType.MESH,
        )
    pl.semaphore_wait(barrier, groups - 1 + shards - 1)
    for copy in small:
        copy.wait()

    cuts = grad_recv.shape[1]
    cut = columns // cuts
    narrow = tile_width(cut, 512)

    def cols_of(c, i):
        return pl.ds(pl.multiple_of(c * cut + i * narrow, narrow), narrow)

    def piece_of(c):
        return pl.ds(pl.multiple_of(c * cut, cut), cut)

    def share_of(expert):
        total = counts[0, expert]
        for s in range(1, groups):
            total = total + counts[s, expert]
        mine = jnp.full((1, LANES), counts[me_group, expert].astype(jnp.float32))
        return (mine / jnp.full((1, LANES), total.astype(jnp.float32)))[:, :1]

    shares = [share_of(peer_of(step)) for step in range(groups)]

    def weighted(step, cols):
        value = shares[step] * grads[step, :, cols].astype(jnp.float32)
        return value.astype(jnp.bfloat16)

    def grad_copy(step, c):
        return remote(
            outgoing.at[step - 1, :, piece_of(c)],
            arrived.at[step - 1, :, piece_of(c)],
            grad_send.at[step - 1, c],
            grad_recv.at[step - 1, c],
            "ep",
            peer_of(step),
        )

    order = sorted(range(1, groups), key=lambda step: abs(2 * step - groups))
    for copy in slabs:
        copy.wait()

    def send_piece(c, carry):
        for step in order:

            def weigh(i, inner, step=step):
                cols = cols_of(c, i)
                outgoing[step - 1, :, cols] = weighted(step, cols)
                return inner

            lax.fori_loop(0, cut // narrow, weigh, 0)
            grad_copy(step, c).start()
        return carry

    lax.fori_loop(0, cuts, send_piece, 0)
    for copy in params:
        copy.wait()


    def moments(c, carry):
        for step in range(1, groups):
            grad_copy(step, c).wait_recv()

        def one(i, inner):
            grad_acc, mom_acc = inner
            cols = cols_of(c, i)
            total = weighted(0, cols).astype(jnp.float32)
            for step in range(1, groups):
                total = total + arrived[step - 1, :, cols].astype(jnp.float32)
            mom_next = MOMENTUM_DECAY * mom[:, cols] + (1.0 - MOMENTUM_DECAY) * total
            gradient[:, cols] = total
            mom[:, cols] = mom_next
            second[:, cols] = (
                SECOND_DECAY * second[:, cols] + (1.0 - SECOND_DECAY) * total * total
            )
            return grad_acc + total * total, mom_acc + mom_next * mom_next

        return lax.fori_loop(0, cut // narrow, one, carry)

    zero = jnp.zeros((rows, narrow), jnp.float32)
    grad_acc, mom_acc = lax.fori_loop(0, cuts, moments, (zero, zero))

    def to_lanes(acc):
        acc = jnp.sum(acc, axis=0, keepdims=True)
        return sum(acc[:, j : j + LANES] for j in range(0, narrow, LANES))

    sums[me, 0:1, :] = to_lanes(grad_acc)
    sums[me, 1:2, :] = to_lanes(mom_acc)
    sum_sends = []
    for step in range(1, shards):
        copy = remote(
            sums.at[me],
            sums.at[me],
            sum_send.at[step - 1],
            sum_recv.at[me],
            "fs",
            (me + step) % shards,
        )
        copy.start()
        sum_sends.append(copy)
    for step in range(1, shards):
        source = (me + step) % shards
        remote(
            sums.at[source],
            sums.at[source],
            sum_send.at[step - 1],
            sum_recv.at[source],
            "fs",
            source,
        ).wait_recv()

    states = [
        pltpu.make_async_copy(mom, mom_hbm_out.at[0], state_sem.at[0]),
        pltpu.make_async_copy(second, second_hbm_out.at[0], state_sem.at[1]),
    ]
    for copy in states:
        copy.start()

    entries = rows * columns * shards
    totals = sums[0]
    for s in range(1, shards):
        totals = totals + sums[s]
    mean = jnp.broadcast_to(jnp.sum(totals, axis=1, keepdims=True) / entries, (2, LANES)) + NORM_EPS
    inverse = lax.rsqrt(mean)
    inv_grad = inverse[0:1, :1]
    inv_mom = inverse[1:2, :1]
    log_mom = jnp.max(0.5 * jnp.log(mean[1:2, :]))
    for h in range(units):
        bias[h] = in_bias[h] + in_weight[5, h] * log_mom

    width = columns // chunks
    tile = tile_width(width, 256)

    def learned_step(cols):
        grad = gradient[:, cols]
        mom_next = mom[:, cols]
        old = weight[:, cols].astype(jnp.float32)
        inv_root = lax.rsqrt(second[:, cols] + ROOT_EPS)
        features = (
            grad * inv_grad,
            mom_next * inv_mom,
            mom_next * inv_root,
            grad * inv_root,
            old,
        )
        direction = jnp.full(grad.shape, out_bias[0])
        magnitude = jnp.full(grad.shape, out_bias[1])
        for h in range(units):
            hidden = features[0] * in_weight[0, h] + bias[h]
            for f in range(1, len(features)):
                hidden = hidden + features[f] * in_weight[f, h]
            hidden = jnp.maximum(hidden, 0.0)
            direction = direction + hidden * out_weight[0, h]
            magnitude = magnitude + hidden * out_weight[1, h]
        update = STEP_SCALE * direction * jnp.exp(EXP_SCALE * magnitude)
        return (old - update).astype(jnp.bfloat16)

    def rows_of(source):
        return pl.ds(pl.multiple_of(source * rows, rows), rows)

    ways = (
        (across, z < depth - 1),
        (-across, z > 0),
        (1, x < across - 1),
        (-1, x > 0),
    )
    turned = turned_chunks(depth, across, chunks)
    along_z = (z, depth, across, (0, 1))
    along_x = (x, across, 1, (2, 3))
    trees = ((along_x, along_z, 0, turned), (along_z, along_x, turned, chunks))

    def block(source, k):
        return gathered.at[rows_of(source), pl.ds(pl.multiple_of(k * width, width), width)]

    def send(tree, source, k, which):
        for number in which:
            offset, possible = ways[number]

            @pl.when(possible)
            def _(number=number, offset=offset):
                piece = block(source, k)
                remote(
                    piece,
                    piece,
                    row_send.at[tree, number, source],
                    row_recv.at[source, k],
                    "fs",
                    me + offset,
                ).start()

    def flush(source, k):
        cols = pl.ds(pl.multiple_of(k * width, width), width)
        pltpu.make_async_copy(
            block(source, k), gathered_hbm.at[0, rows_of(source), cols], flush_sem.at[source]
        ).start()

    def await_block(source, k):
        piece = block(source, k)
        remote(
            piece, piece, row_send.at[0, 0, source], row_recv.at[source, k], "fs", source
        ).wait_recv()

    def relay(t, tree):
        first, second, low, high = trees[tree]
        if low == high:
            return
        at, size, stride, (up, down) = first
        for d in range(1, size):
            k = t - LAG * d
            live = jnp.logical_and(k >= low, k < high)

            @pl.when(jnp.logical_and(live, at >= d))
            def _(d=d, k=k):
                source = me - d * stride
                await_block(source, k)
                send(tree, source, k, (up,) + second[3])
                flush(source, k)

            @pl.when(jnp.logical_and(live, at + d < size))
            def _(d=d, k=k):
                source = me + d * stride
                await_block(source, k)
                send(tree, source, k, (down,) + second[3])
                flush(source, k)

        other, length, pitch, (up_other, down_other) = second
        for e in range(1, length):
            k = t - LAG * (size - 1 + e)
            live = jnp.logical_and(k >= low, k < high)
            for level in range(size):

                @pl.when(jnp.logical_and(live, other >= e))
                def _(e=e, k=k, level=level):
                    source = level * stride + (other - e) * pitch
                    await_block(source, k)
                    send(tree, source, k, (up_other,))
                    flush(source, k)

                @pl.when(jnp.logical_and(live, other + e < length))
                def _(e=e, k=k, level=level):
                    source = level * stride + (other + e) * pitch
                    await_block(source, k)
                    send(tree, source, k, (down_other,))
                    flush(source, k)

    def turn(t, carry):
        @pl.when(t < chunks)
        def _():
            def one(i, inner):
                cols = pl.ds(pl.multiple_of(t * width + i * tile, tile), tile)
                gathered[rows_of(me), cols] = learned_step(cols)
                return inner

            lax.fori_loop(0, width // tile, one, 0)

        for tree in range(2):
            _, _, low, high = trees[tree]

            @pl.when(jnp.logical_and(t >= low, t < high))
            def _(tree=tree):
                send(tree, me, t, (0, 1, 2, 3))
                flush(me, t)

        for tree in range(2):
            relay(t, tree)
        return carry

    lax.fori_loop(0, chunks + LAG * (depth - 1 + across - 1), turn, 0)

    def drain(c, carry):
        for step in range(1, groups):
            grad_copy(step, c).wait_send()
        return carry

    lax.fori_loop(0, cuts, drain, 0)
    for copy in sum_sends:
        copy.wait_send()
    for copy in states:
        copy.wait()
    for source in range(shards):
        pltpu.make_async_copy(
            gathered.at[rows_of(source), :],
            gathered_hbm.at[0, rows_of(source), :],
            flush_sem.at[source],
        ).wait()
    for tree in range(2):
        first, _, low, high = trees[tree]
        if low == high:
            continue
        for number, (_, possible) in enumerate(ways):
            for source in range(shards):
                level, place = source // across, source % across
                used = (level <= z, level >= z, place <= x, place >= x)[number]
                if first is along_z and number < 2:
                    used = jnp.logical_and(used, place == x)
                if first is along_x and number >= 2:
                    used = jnp.logical_and(used, level == z)

                @pl.when(jnp.logical_and(possible, used))
                def _(tree=tree, number=number, source=source, low=low, high=high):
                    piece = gathered.at[rows_of(source), pl.ds(low * width, (high - low) * width)]
                    remote(
                        piece,
                        piece,
                        row_send.at[tree, number, source],
                        row_recv.at[source, low],
                        "fs",
                        (me + 1) % shards,
                    ).wait_send()


def per_device(
    groups, shards, grads, counts, weight, mom, second, in_weight, in_bias, out_weight, out_bias
):
    rows, columns = mom.shape[1], mom.shape[2]
    across = max(d for d in range(1, shards + 1) if shards % d == 0 and d * d <= shards)
    depth = shards // across
    chunks = largest_divisor(columns // LANES, MOST_CHUNKS)
    cuts = largest_divisor(columns // LANES, MOST_CUTS)
    hbm = pl.BlockSpec(memory_space=pltpu.HBM)
    return pl.pallas_call(
        functools.partial(kernel, groups, depth, across, chunks),
        out_shape=(
            jax.ShapeDtypeStruct((1, rows * shards, columns), jnp.bfloat16),
            jax.ShapeDtypeStruct(mom.shape, jnp.float32),
            jax.ShapeDtypeStruct(second.shape, jnp.float32),
        ),
        in_specs=[hbm] * 9,
        out_specs=(hbm, hbm, hbm),
        scratch_shapes=[
            pltpu.SMEM(counts.shape, jnp.int32),
            pltpu.SMEM(in_weight.shape, jnp.float32),
            pltpu.SMEM(in_bias.shape, jnp.float32),
            pltpu.SMEM(out_weight.shape[::-1], jnp.float32),
            pltpu.SMEM(out_bias.shape, jnp.float32),
            pltpu.VMEM((groups, rows, columns), jnp.bfloat16),
            pltpu.VMEM((rows, columns), jnp.bfloat16),
            pltpu.VMEM((rows, columns), jnp.float32),
            pltpu.VMEM((rows, columns), jnp.float32),
            pltpu.VMEM((rows * shards, columns), jnp.bfloat16),
            pltpu.VMEM((groups - 1, rows, columns), jnp.bfloat16),
            pltpu.VMEM((groups - 1, rows, columns), jnp.bfloat16),
            pltpu.VMEM((rows, columns), jnp.float32),
            pltpu.VMEM((shards, 2, LANES), jnp.float32),
            pltpu.SMEM((in_bias.shape[0],), jnp.float32),
            pltpu.SemaphoreType.DMA((5,)),
            pltpu.SemaphoreType.DMA((groups,)),
            pltpu.SemaphoreType.DMA((3,)),
            pltpu.SemaphoreType.DMA((groups - 1, cuts)),
            pltpu.SemaphoreType.DMA((groups - 1, cuts)),
            pltpu.SemaphoreType.DMA((shards,)),
            pltpu.SemaphoreType.DMA((2,)),
            pltpu.SemaphoreType.DMA((shards - 1,)),
            pltpu.SemaphoreType.DMA((shards,)),
            pltpu.SemaphoreType.DMA((2, 4, shards)),
            pltpu.SemaphoreType.DMA((shards, chunks)),
        ],
        compiler_params=pltpu.CompilerParams(
            collective_id=0, has_side_effects=True, vmem_limit_bytes=VMEM_BYTES
        ),
        name="learned_update",
    )(counts, in_weight, in_bias, out_weight.T, out_bias, grads, weight, mom, second)


def solution(mesh):
    in_specs = (
        P("ep", None, "fs", None),
        P(),
        P("ep", "fs", None),
        P("ep", "fs", None),
        P("ep", "fs", None),
        P(),
        P(),
        P(),
        P(),
    )
    out_specs = (P("ep", None, None), P("ep", "fs", None), P("ep", "fs", None))
    body = functools.partial(per_device, mesh.shape["ep"], mesh.shape["fs"])
    return jax.shard_map(
        body, mesh=mesh, in_specs=in_specs, out_specs=out_specs, check_vma=False
    )
```

profile of v0, /device:TPU:0, one launch (start us, length us, event | category | flops | bytes accessed | tf_op | source)
XLA Modules:
  0.0 83.2 jit_solution(16970597023861139422)
XLA Ops:
  0.6 76.4 %learned_update.1 = (bf16[1,128,14336]{2,1,0:T(8,128)(2,1)}, f32[1,16,14336]{2,1,0:T(8,128)}, f32[1,16,14336]{2,1,0:T(8,128)}) custom-call(s32[4,4]{1,0:T(4,128)} %counts_hbm.1, f32[6,32]{1,0:T(8,128)} %in_weight_hbm.1, f32[32]{0:T(128)} %in_bias_hbm.1, f32[2,32]{1,0:T(2,128)} %bitcast.1, f32[2]{0:T(128)} %out_bias_hbm.1, ...), custom_call_target="tpu_custom_call" | custom-call | tf_op jit(solution)/shard_map/learned_update/pallas_call | solution.py:477
  77.0 0.0 copy-start.1
  77.1 0.0 copy-start
  77.1 4.3 %copy.15 = bf16[1,128,14336]{2,1,0:T(8,128)(2,1)} copy(bf16[1,128,14336]{2,1,0:T(8,128)(2,1)} %get-tuple-element.6) | data formatting | bytes 7340032
  81.4 0.0 copy-done.1
  81.4 0.9 %copy.16 = f32[1,16,14336]{2,1,0:T(8,128)} copy(f32[1,16,14336]{2,1,0:T(8,128)S(1)} %copy-done.1) | data formatting | bytes 1835008
  82.3 0.0 copy-done
  82.3 0.9 %copy.17 = f32[1,16,14336]{2,1,0:T(8,128)} copy(f32[1,16,14336]{2,1,0:T(8,128)S(1)} %copy-done) | data formatting | bytes 1835008
Async XLA Ops:
  77.0 4.4 %copy-start.1 = (f32[1,16,14336]{2,1,0:T(8,128)S(1)}, f32[1,16,14336]{2,1,0:T(8,128)}, u32[]{:S(2)}) copy-start(f32[1,16,14336]{2,1,0:T(8,128)} %get-tuple-element.7) | copy-start | bytes 2752516
  77.1 5.3 %copy-start = (f32[1,16,14336]{2,1,0:T(8,128)S(1)}, f32[1,16,14336]{2,1,0:T(8,128)}, u32[]{:S(2)}) copy-start(f32[1,16,14336]{2,1,0:T(8,128)} %get-tuple-element.8) | copy-start | bytes 2752516
where the time goes:
time: 83.4 us; the launch traced here: 83.2 us
  Pallas kernels  76.4 us (92%)
  local copies, waits for them, and re-layouts  6.18 us (7%)
    pallas_call x1, Pallas kernels, per_device(): pl.pallas_call(functools.partial(kernel, groups, depth, across, chunks),...  76.4 us
    unnamed x7, local copies, waits for them, and re-layouts  6.18 us

commit v1 on v0

v1 whole, which is shorter than its diff:
```python
import functools

import jax
import jax.numpy as jnp
from jax import lax
from jax.experimental import pallas as pl
from jax.experimental.pallas import tpu as pltpu
from jax.sharding import PartitionSpec as P

MOMENTUM_DECAY = 0.9
SECOND_DECAY = 0.99
NORM_EPS = 1e-06
ROOT_EPS = 1e-08
STEP_SCALE = 0.2
EXP_SCALE = 0.5
LANES = 128
CORES = 2
MOST_CHUNKS = 28
MOST_CUTS = 14
LAG = 4
TURN_LAG = 4
VMEM_BYTES = 67043328
FLUSH_BYTES = 1 << 20


def largest_divisor(number, most):
    return max(d for d in range(1, most + 1) if number % d == 0)


def tile_width(columns, most):
    return LANES * largest_divisor(columns // LANES, most // LANES)


def turned_chunks(depth, across, chunks):
    def load(turned):
        straight = chunks - turned
        on_x = (across - 1) * (depth * straight + turned)
        on_z = (depth - 1) * (straight + across * turned)
        return max(on_x, on_z)

    return min(range(chunks + 1), key=load)


def remote(src, dst, send_sem, recv_sem, axis, peer):
    return pltpu.make_async_remote_copy(
        src_ref=src,
        dst_ref=dst,
        send_sem=send_sem,
        recv_sem=recv_sem,
        device_id={axis: peer},
        device_id_type=pl.DeviceIdType.MESH,
    )


def signal(semaphore, axis, peer):
    pl.semaphore_signal(
        semaphore, inc=1, device_id={axis: peer}, device_id_type=pl.DeviceIdType.MESH
    )


def kernel(
    groups,
    depth,
    across,
    chunks,
    counts_hbm,
    in_weight_hbm,
    in_bias_hbm,
    out_weight_hbm,
    out_bias_hbm,
    grads_hbm,
    weight_hbm,
    mom_hbm,
    second_hbm,
    gathered,
    mom,
    second,
    counts,
    in_weight,
    in_bias,
    out_weight,
    out_bias,
    grads,
    weight,
    handed,
    taken,
    outgoing,
    arrived,
    gradient,
    sums,
    bias,
    small_sem,
    slab_sem,
    param_sem,
    pair_send,
    pair_recv,
    grad_send,
    grad_recv,
    chain,
    sum_send,
    sum_recv,
    row_send,
    row_recv,
):
    shards = depth * across
    planes = groups // CORES
    rows, columns = mom.shape
    units = in_bias.shape[0]
    me_group = lax.axis_index("ep")
    plane = me_group // CORES
    core = me_group % CORES
    partner = plane * CORES + (CORES - 1 - core)
    me = lax.axis_index("fs")
    z = me // across
    x = me % across

    def own_of(step):
        return (plane + step) % planes * CORES + core

    def other_of(step):
        return (plane + step) % planes * CORES + (CORES - 1 - core)

    barrier = pltpu.get_barrier_semaphore()
    signal(barrier, "ep", partner)
    for step in range(1, planes):
        signal(barrier, "ep", own_of(step))
    for step in range(1, across):
        signal(barrier, "fs", z * across + (x + step) % across)

    @pl.when(z < depth - 1)
    def _():
        signal(barrier, "fs", me + across)

    @pl.when(z > 0)
    def _():
        signal(barrier, "fs", me - across)

    small = [
        pltpu.make_async_copy(src, dst, small_sem.at[i])
        for i, (src, dst) in enumerate(
            (
                (counts_hbm, counts),
                (in_weight_hbm, in_weight),
                (in_bias_hbm, in_bias),
                (out_weight_hbm, out_weight),
                (out_bias_hbm, out_bias),
            )
        )
    ]
    for copy in small:
        copy.start()

    order = [*range(1, planes), 0]
    slabs = [
        pltpu.make_async_copy(
            grads_hbm.at[0, expert_of(step)], grads.at[kind, step], slab_sem.at[kind, step]
        )
        for kind, expert_of in enumerate((other_of, own_of))
        for step in order
    ]
    for copy in slabs:
        copy.start()
    params = [
        pltpu.make_async_copy(src.at[0], dst, param_sem.at[i])
        for i, (src, dst) in enumerate(
            (
                (mom_hbm, mom),
                (second_hbm, second),
                (weight_hbm, weight),
            )
        )
    ]
    for copy in params:
        copy.start()

    cuts = grad_recv.shape[1]
    cut = columns // cuts
    narrow = tile_width(cut, 512)

    def cols_of(c, i):
        return pl.ds(pl.multiple_of(c * cut + i * narrow, narrow), narrow)

    def piece_of(c):
        return pl.ds(pl.multiple_of(c * cut, cut), cut)

    for copy in small:
        copy.wait()

    def share_of(expert):
        total = counts[0, expert]
        for s in range(1, groups):
            total = total + counts[s, expert]
        mine = jnp.full((1, LANES), counts[me_group, expert].astype(jnp.float32))
        return (mine / jnp.full((1, LANES), total.astype(jnp.float32)))[:, :1]

    shares = [
        [share_of(expert_of(step)) for step in range(planes)] for expert_of in (other_of, own_of)
    ]

    def weighted(kind, step, cols):
        value = shares[kind][step] * grads[kind, step, :, cols].astype(jnp.float32)
        return value.astype(jnp.bfloat16)

    for copy in slabs[:planes]:
        copy.wait()

    def hand(i, carry):
        cols = pl.ds(pl.multiple_of(i * narrow, narrow), narrow)
        for step in order:
            handed[step, :, cols] = weighted(0, step, cols)
        return carry

    lax.fori_loop(0, columns // narrow, hand, 0)
    for copy in slabs[planes:]:
        copy.wait()

    near = 1 + (planes - 1) + (across - 1)
    near = near + (z > 0).astype(jnp.int32) + (z < depth - 1).astype(jnp.int32)
    pl.semaphore_wait(barrier, near)

    def pair_copy(step, c):
        return remote(
            handed.at[step, :, piece_of(c)],
            taken.at[step, :, piece_of(c)],
            pair_send.at[step, c],
            pair_recv.at[step, c],
            "ep",
            partner,
        )

    def grad_copy(step, c):
        return remote(
            outgoing.at[step - 1, :, piece_of(c)],
            arrived.at[step - 1, :, piece_of(c)],
            grad_send.at[step - 1, c],
            grad_recv.at[step - 1, c],
            "ep",
            own_of(step),
        )

    def start_pairs(c, carry):
        for step in order[:-1]:
            pair_copy(step, c).start()
        return carry

    lax.fori_loop(0, cuts, start_pairs, 0)

    def start_own(c, carry):
        pair_copy(0, c).start()
        return carry

    lax.fori_loop(0, cuts, start_own, 0)

    def send_piece(c, carry):
        for step in order[:-1]:
            pair_copy(step, c).wait_recv()

            def add(i, inner, step=step):
                cols = cols_of(c, i)
                total = weighted(1, step, cols).astype(jnp.float32)
                total = total + taken[step, :, cols].astype(jnp.float32)
                outgoing[step - 1, :, cols] = total.astype(jnp.bfloat16)
                return inner

            lax.fori_loop(0, cut // narrow, add, 0)
            grad_copy(step, c).start()
        return carry

    lax.fori_loop(0, cuts, send_piece, 0)

    @pl.when(z > 0)
    def _():
        pl.semaphore_wait(chain.at[0], 1)

    @pl.when(z < depth - 1)
    def _():
        signal(chain.at[0], "fs", me + across)
        pl.semaphore_wait(chain.at[1], 1)

    @pl.when(z > 0)
    def _():
        signal(chain.at[1], "fs", me - across)

    def gather_own(c, carry):
        pair_copy(0, c).wait_recv()

        def one(i, inner):
            cols = cols_of(c, i)
            gradient[:, cols] = weighted(1, 0, cols).astype(jnp.float32) + taken[
                0, :, cols
            ].astype(jnp.float32)
            return inner

        return lax.fori_loop(0, cut // narrow, one, carry)

    lax.fori_loop(0, cuts, gather_own, 0)
    for copy in params:
        copy.wait()

    def moments(c, carry):
        for step in range(1, planes):
            grad_copy(step, c).wait_recv()

        def one(i, inner):
            grad_acc, mom_acc = inner
            cols = cols_of(c, i)
            total = gradient[:, cols]
            for step in range(1, planes):
                total = total + arrived[step - 1, :, cols].astype(jnp.float32)
            mom_next = MOMENTUM_DECAY * mom[:, cols] + (1.0 - MOMENTUM_DECAY) * total
            gradient[:, cols] = total
            mom[:, cols] = mom_next
            second[:, cols] = (
                SECOND_DECAY * second[:, cols] + (1.0 - SECOND_DECAY) * total * total
            )
            return grad_acc + total * total, mom_acc + mom_next * mom_next

        return lax.fori_loop(0, cut // narrow, one, carry)

    zero = jnp.zeros((rows, narrow), jnp.float32)
    grad_acc, mom_acc = lax.fori_loop(0, cuts, moments, (zero, zero))

    def to_lanes(acc):
        acc = jnp.sum(acc, axis=0, keepdims=True)
        return sum(acc[:, j : j + LANES] for j in range(0, narrow, LANES))

    sums[me, 0:1, :] = to_lanes(grad_acc)
    sums[me, 1:2, :] = to_lanes(mom_acc)
    sum_sends = []
    for step in range(1, shards):
        copy = remote(
            sums.at[me],
            sums.at[me],
            sum_send.at[step - 1],
            sum_recv.at[me],
            "fs",
            (me + step) % shards,
        )
        copy.start()
        sum_sends.append(copy)
    for step in range(1, shards):
        source = (me + step) % shards
        remote(
            sums.at[source],
            sums.at[source],
            sum_send.at[step - 1],
            sum_recv.at[source],
            "fs",
            source,
        ).wait_recv()

    entries = rows * columns * shards
    totals = sums[0]
    for s in range(1, shards):
        totals = totals + sums[s]
    mean = jnp.broadcast_to(jnp.sum(totals, axis=1, keepdims=True) / entries, (2, LANES)) + NORM_EPS
    inverse = lax.rsqrt(mean)
    inv_grad = inverse[0:1, :1]
    inv_mom = inverse[1:2, :1]
    log_mom = jnp.max(0.5 * jnp.log(mean[1:2, :]))
    for h in range(units):
        bias[h] = in_bias[h] + in_weight[5, h] * log_mom

    width = columns // chunks
    tile = tile_width(width, 256)

    def learned_step(cols):
        grad = gradient[:, cols]
        mom_next = mom[:, cols]
        old = weight[:, cols].astype(jnp.float32)
        inv_root = lax.rsqrt(second[:, cols] + ROOT_EPS)
        features = (
            grad * inv_grad,
            mom_next * inv_mom,
            mom_next * inv_root,
            grad * inv_root,
            old,
        )
        direction = jnp.full(grad.shape, out_bias[0])
        magnitude = jnp.full(grad.shape, out_bias[1])
        for h in range(units):
            hidden = features[0] * in_weight[0, h] + bias[h]
            for f in range(1, len(features)):
                hidden = hidden + features[f] * in_weight[f, h]
            hidden = jnp.maximum(hidden, 0.0)
            direction = direction + hidden * out_weight[0, h]
            magnitude = magnitude + hidden * out_weight[1, h]
        update = STEP_SCALE * direction * jnp.exp(EXP_SCALE * magnitude)
        return (old - update).astype(jnp.bfloat16)

    def rows_of(source):
        return pl.ds(pl.multiple_of(source * rows, rows), rows)

    ways = (
        (across, z < depth - 1),
        (-across, z > 0),
        (1, x < across - 1),
        (-1, x > 0),
    )
    turned = turned_chunks(depth, across, chunks)
    period = chunks // turned if turned else chunks
    along_z = (z, depth, across, (0, 1))
    along_x = (x, across, 1, (2, 3))
    trees = ((along_x, along_z, turned), (along_z, along_x, chunks - turned))

    def in_tree(tree, k):
        if not turned:
            return k >= 0 if tree else k < 0
        chosen = jnp.logical_and(k % period == period // 2, k // period < turned)
        return jnp.logical_not(chosen) if tree else chosen

    def block(source, k):
        return gathered.at[rows_of(source), pl.ds(pl.multiple_of(k * width, width), width)]

    def send(tree, source, k, which):
        for number in which:
            offset, possible = ways[number]

            @pl.when(possible)
            def _(number=number, offset=offset):
                piece = block(source, k)
                remote(
                    piece,
                    piece,
                    row_send.at[tree, number, source],
                    row_recv.at[source, k],
                    "fs",
                    me + offset,
                ).start()

    def await_block(source, k):
        piece = block(source, k)
        remote(
            piece, piece, row_send.at[0, 0, source], row_recv.at[source, k], "fs", source
        ).wait_recv()

    def live(tree, k):
        inside = jnp.logical_and(k >= 0, k < chunks)
        return jnp.logical_and(inside, in_tree(tree, jnp.maximum(k, 0)))

    def relay(t, tree):
        first, second, count = trees[tree]
        if not count:
            return
        at, size, stride, (up, down) = first
        other, length, pitch, (up_other, down_other) = second
        lag = LAG if tree else TURN_LAG
        for d in range(size - 1, 0, -1):
            k = t - lag * d

            @pl.when(live(tree, k))
            def _(d=d, k=k):
                @pl.when(at >= d)
                def _():
                    source = me - d * stride
                    await_block(source, k)
                    send(tree, source, k, (up,) + second[3])

                @pl.when(at + d < size)
                def _():
                    source = me + d * stride
                    await_block(source, k)
                    send(tree, source, k, (down,) + second[3])

        for e in range(length - 2, 0, -1):
            k = t - lag * (size - 1) - LAG * e

            @pl.when(live(tree, k))
            def _(e=e, k=k):
                for level in range(size):

                    @pl.when(jnp.logical_and(other >= e, other < length - 1))
                    def _(level=level):
                        source = level * stride + (other - e) * pitch
                        await_block(source, k)
                        send(tree, source, k, (up_other,))

                    @pl.when(jnp.logical_and(other + e < length, other > 0))
                    def _(level=level):
                        source = level * stride + (other + e) * pitch
                        await_block(source, k)
                        send(tree, source, k, (down_other,))

    def turn(t, carry):
        @pl.when(t < chunks)
        def _():
            def one(i, inner):
                cols = pl.ds(pl.multiple_of(t * width + i * tile, tile), tile)
                gathered[rows_of(me), cols] = learned_step(cols)
                return inner

            lax.fori_loop(0, width // tile, one, 0)

        for tree in range(2):

            @pl.when(live(tree, t))
            def _(tree=tree):
                send(tree, me, t, (0, 1, 2, 3))

        for tree in (1, 0):
            relay(t, tree)
        return carry

    reach = max(
        LAG * (depth - 1) + LAG * max(across - 2, 0),
        TURN_LAG * (across - 1) + LAG * max(depth - 2, 0),
    )
    lax.fori_loop(0, chunks + reach, turn, 0)

    def finish(k, carry):
        for tree in range(2):
            first, second, count = trees[tree]
            _, size, stride, _ = first
            other, length, pitch, _ = second

            @pl.when(in_tree(tree, k))
            def _(size=size, stride=stride, other=other, length=length, pitch=pitch):
                for level in range(size):
                    for place in range(length):
                        below = jnp.logical_and(place < other, other == length - 1)
                        above = jnp.logical_and(place > other, other == 0)

                        @pl.when(jnp.logical_or(below, above))
                        def _(level=level, place=place):
                            await_block(level * stride + place * pitch, k)

        return carry

    lax.fori_loop(0, chunks, finish, 0)

    def drain(c, carry):
        for step in range(planes):
            pair_copy(step, c).wait_send()
        for step in range(1, planes):
            grad_copy(step, c).wait_send()
        return carry

    lax.fori_loop(0, cuts, drain, 0)
    for copy in sum_sends:
        copy.wait_send()
    for tree in range(2):
        first, _, count = trees[tree]
        if not count:
            continue
        for number, (_, possible) in enumerate(ways):
            for source in range(shards):
                level, place = source // across, source % across
                used = (level <= z, level >= z, place <= x, place >= x)[number]
                if first is along_z and number < 2:
                    used = jnp.logical_and(used, place == x)
                if first is along_x and number >= 2:
                    used = jnp.logical_and(used, level == z)

                @pl.when(jnp.logical_and(possible, used))
                def _(tree=tree, number=number, source=source, count=count):
                    piece = gathered.at[rows_of(source), pl.ds(0, count * width)]
                    remote(
                        piece,
                        piece,
                        row_send.at[tree, number, source],
                        row_recv.at[source, 0],
                        "fs",
                        (me + 1) % shards,
                    ).wait_send()


def flush(gathered, mom, second, gathered_hbm, mom_hbm, second_hbm, sem):
    copies = []
    for i, (src, dst) in enumerate(
        ((gathered, gathered_hbm), (mom, mom_hbm), (second, second_hbm))
    ):
        height = src.shape[0] // largest_divisor(src.shape[0] // 16, 8)
        for n in range(src.shape[0] // height):
            rows = pl.ds(n * height, height)
            copies.append(
                pltpu.make_async_copy(src.at[rows], dst.at[0, rows], sem.at[len(copies)])
            )
    for copy in copies:
        copy.start()
    for copy in copies:
        copy.wait()


def per_device(
    groups, shards, grads, counts, weight, mom, second, in_weight, in_bias, out_weight, out_bias
):
    rows, columns = mom.shape[1], mom.shape[2]
    across = max(d for d in range(1, shards + 1) if shards % d == 0 and d * d <= shards)
    depth = shards // across
    planes = groups // CORES
    chunks = largest_divisor(columns // LANES, MOST_CHUNKS)
    cuts = largest_divisor(columns // LANES, MOST_CUTS)
    hbm = pl.BlockSpec(memory_space=pltpu.HBM)
    vmem = pl.BlockSpec(memory_space=pltpu.VMEM)
    held = (2 * shards + 8) * rows * columns
    gathered, new_mom, new_second = pl.pallas_call(
        functools.partial(kernel, groups, depth, across, chunks),
        out_shape=(
            pltpu.VMEM((rows * shards, columns), jnp.bfloat16),
            pltpu.VMEM((rows, columns), jnp.float32),
            pltpu.VMEM((rows, columns), jnp.float32),
        ),
        in_specs=[hbm] * 9,
        out_specs=(vmem, vmem, vmem),
        scratch_shapes=[
            pltpu.SMEM(counts.shape, jnp.int32),
            pltpu.SMEM(in_weight.shape, jnp.float32),
            pltpu.SMEM(in_bias.shape, jnp.float32),
            pltpu.SMEM(out_weight.shape[::-1], jnp.float32),
            pltpu.SMEM(out_bias.shape, jnp.float32),
            pltpu.VMEM((CORES, planes, rows, columns), jnp.bfloat16),
            pltpu.VMEM((rows, columns), jnp.bfloat16),
            pltpu.VMEM((planes, rows, columns), jnp.bfloat16),
            pltpu.VMEM((planes, rows, columns), jnp.bfloat16),
            pltpu.VMEM((planes - 1, rows, columns), jnp.bfloat16),
            pltpu.VMEM((planes - 1, rows, columns), jnp.bfloat16),
            pltpu.VMEM((rows, columns), jnp.float32),
            pltpu.VMEM((shards, 2, LANES), jnp.float32),
            pltpu.SMEM((in_bias.shape[0],), jnp.float32),
            pltpu.SemaphoreType.DMA((5,)),
            pltpu.SemaphoreType.DMA((CORES, planes)),
            pltpu.SemaphoreType.DMA((3,)),
            pltpu.SemaphoreType.DMA((planes, cuts)),
            pltpu.SemaphoreType.DMA((planes, cuts)),
            pltpu.SemaphoreType.DMA((planes - 1, cuts)),
            pltpu.SemaphoreType.DMA((planes - 1, cuts)),
            pltpu.SemaphoreType.REGULAR((2,)),
            pltpu.SemaphoreType.DMA((shards - 1,)),
            pltpu.SemaphoreType.DMA((shards,)),
            pltpu.SemaphoreType.DMA((2, 4, shards)),
            pltpu.SemaphoreType.DMA((shards, chunks)),
        ],
        compiler_params=pltpu.CompilerParams(
            collective_id=0,
            has_side_effects=True,
            vmem_limit_bytes=VMEM_BYTES - held,
        ),
        name="learned_update",
    )(counts, in_weight, in_bias, out_weight.T, out_bias, grads, weight, mom, second)
    return pl.pallas_call(
        flush,
        out_shape=(
            jax.ShapeDtypeStruct((1, rows * shards, columns), jnp.bfloat16),
            jax.ShapeDtypeStruct(mom.shape, jnp.float32),
            jax.ShapeDtypeStruct(second.shape, jnp.float32),
        ),
        in_specs=[vmem] * 3,
        out_specs=(hbm, hbm, hbm),
        scratch_shapes=[pltpu.SemaphoreType.DMA((24,))],
        compiler_params=pltpu.CompilerParams(
            has_side_effects=True, vmem_limit_bytes=FLUSH_BYTES
        ),
        name="flush",
    )(gathered, new_mom, new_second)


def solution(mesh):
    in_specs = (
        P("ep", None, "fs", None),
        P(),
        P("ep", "fs", None),
        P("ep", "fs", None),
        P("ep", "fs", None),
        P(),
        P(),
        P(),
        P(),
    )
    out_specs = (P("ep", None, None), P("ep", "fs", None), P("ep", "fs", None))
    body = functools.partial(per_device, mesh.shape["ep"], mesh.shape["fs"])
    return jax.shard_map(
        body, mesh=mesh, in_specs=in_specs, out_specs=out_specs, check_vma=False
    )
```

time: 83.4 us -> 71.7 us (0.86)
  local copies, waits for them, and re-layouts: 6.18 us -> 0 us
  Pallas kernels: 76.4 us -> 70.8 us
    pallas_call x1, Pallas kernels: 76.4 us -> 68.2 us  [per_device(): pl.pallas_call(functools.partial(kernel, groups, depth, across, chunks),...]
    unnamed x7 -> x0, local copies, waits for them, and re-layouts: 6.18 us -> none
    pallas_call x0 -> x1, Pallas kernels: none -> 2.65 us  [per_device(): pl.pallas_call(flush, out_shape=(jax.ShapeDtypeStruct((1, rows * shards,...]
where the time goes in v1:
time: 71.7 us; the launch traced here: 71.5 us
  Pallas kernels  70.8 us (99%)
    pallas_call x1, Pallas kernels, per_device(): pl.pallas_call(functools.partial(kernel, groups, depth, across, chunks),...  68.2 us
    pallas_call x1, Pallas kernels, per_device(): pl.pallas_call(flush, out_shape=(jax.ShapeDtypeStruct((1, rows * shards,...  2.65 us

profile of v1, /device:TPU:0, one launch (start us, length us, event | category | flops | bytes accessed | tf_op | source)
XLA Modules:
  0.0 71.5 jit_solution(9130570728522111640)
XLA Ops:
  0.6 68.2 %learned_update.1 = (bf16[128,14336]{1,0:T(8,128)(2,1)S(1)}, f32[16,14336]{1,0:T(8,128)S(1)}, f32[16,14336]{1,0:T(8,128)S(1)}) custom-call(s32[4,4]{1,0:T(4,128)} %counts_hbm.1, f32[6,32]{1,0:T(8,128)} %in_weight_hbm.1, f32[32]{0:T(128)} %in_bias_hbm.1, f32[2,32]{1,0:T(2,128)} %bitcast.1, f32[2]{0:T(128)} %out_bias_hbm.1, ...), custom_call_target="tpu_custom_call" | custom-call | tf_op jit(solution)/shard_map/learned_update/pallas_call | solution.py:596
  68.8 2.6 %flush.1 = (bf16[1,128,14336]{2,1,0:T(8,128)(2,1)}, f32[1,16,14336]{2,1,0:T(8,128)}, f32[1,16,14336]{2,1,0:T(8,128)}) custom-call(bf16[128,14336]{1,0:T(8,128)(2,1)S(1)} %get-tuple-element.6.gathered, f32[16,14336]{1,0:T(8,128)S(1)} %get-tuple-element.7.mom, f32[16,14336]{1,0:T(8,128)S(1)} %get-tuple-element.8.second), custom_call_target="tpu_custom_call" | custom-call | tf_op jit(solution)/shard_map/flush/pallas_call | solution.py:640

commit v2 on v1

--- a/solution.py
+++ b/solution.py
@@ -15,10 +15,13 @@
 EXP_SCALE = 0.5
 LANES = 128
 CORES = 2
-MOST_CHUNKS = 28
-MOST_CUTS = 14
-LAG = 4
-TURN_LAG = 4
+MOST_CHUNKS = 14
+MOST_CUTS = 7
+CODE_SCALE = 512.0
+CODE_LEAST = 2.0**-126
+GO_EARLY = 3
+LAG = 3
+TURN_LAG = 3
 VMEM_BYTES = 67043328
 FLUSH_BYTES = 1 << 20
 
@@ -50,6 +53,20 @@
         device_id={axis: peer},
         device_id_type=pl.DeviceIdType.MESH,
     )
+
+
+def coded(value):
+    power = value * CODE_SCALE
+    for _ in range(3):
+        power = power * power
+    return jnp.where(value < 0.0, -power, power).astype(jnp.bfloat16)
+
+
+def decoded(code):
+    code = code.astype(jnp.float32)
+    fourth = lax.rsqrt(lax.rsqrt(jnp.maximum(jnp.abs(code), CODE_LEAST)))
+    size = fourth * lax.rsqrt(fourth) * (1.0 / CODE_SCALE)
+    return jnp.where(code == 0.0, 0.0, jnp.where(code < 0.0, -size, size))
 
 
 def signal(semaphore, axis, peer):
@@ -94,13 +111,16 @@
     param_sem,
     pair_send,
     pair_recv,
+    own_recv,
     grad_send,
     grad_recv,
     chain,
-    sum_send,
-    sum_recv,
+    go,
+    sum_sem,
     row_send,
-    row_recv,
+    near_recv,
+    turned_recv,
+    straight_recv,
 ):
     shards = depth * across
     planes = groups // CORES
@@ -151,15 +171,17 @@
         copy.start()
 
     order = [*range(1, planes), 0]
-    slabs = [
+    for kind, expert_of in enumerate((other_of, own_of)):
+        for step in order:
+            pltpu.make_async_copy(
+                grads_hbm.at[0, expert_of(step)], grads.at[kind, step], slab_sem.at[kind]
+            ).start()
+
+    def await_slabs(kind):
         pltpu.make_async_copy(
-            grads_hbm.at[0, expert_of(step)], grads.at[kind, step], slab_sem.at[kind, step]
-        )
-        for kind, expert_of in enumerate((other_of, own_of))
-        for step in order
-    ]
-    for copy in slabs:
-        copy.start()
+            grads_hbm.at[0, pl.ds(0, planes)], grads.at[kind], slab_sem.at[kind]
+        ).wait()
+
     params = [
         pltpu.make_async_copy(src.at[0], dst, param_sem.at[i])
         for i, (src, dst) in enumerate(
@@ -175,7 +197,7 @@
 
     cuts = grad_recv.shape[1]
     cut = columns // cuts
-    narrow = tile_width(cut, 512)
+    narrow = tile_width(cut, 1024)
 
     def cols_of(c, i):
         return pl.ds(pl.multiple_of(c * cut + i * narrow, narrow), narrow)
@@ -201,8 +223,7 @@
         value = shares[kind][step] * grads[kind, step, :, cols].astype(jnp.float32)
         return value.astype(jnp.bfloat16)
 
-    for copy in slabs[:planes]:
-        copy.wait()
+    await_slabs(0)
 
     def hand(i, carry):
         cols = pl.ds(pl.multiple_of(i * narrow, narrow), narrow)
@@ -211,8 +232,7 @@
         return carry
 
     lax.fori_loop(0, columns // narrow, hand, 0)
-    for copy in slabs[planes:]:
-        copy.wait()
+    await_slabs(1)
 
     near = 1 + (planes - 1) + (across - 1)
     near = near + (z > 0).astype(jnp.int32) + (z < depth - 1).astype(jnp.int32)
@@ -222,17 +242,19 @@
         return remote(
             handed.at[step, :, piece_of(c)],
             taken.at[step, :, piece_of(c)],
-            pair_send.at[step, c],
-            pair_recv.at[step, c],
+            pair_send,
+            pair_recv.at[step - 1, c],
             "ep",
             partner,
         )
+
+    own_copy = remote(handed.at[0], taken.at[0], pair_send, own_recv, "ep", partner)
 
     def grad_copy(step, c):
         return remote(
             outgoing.at[step - 1, :, piece_of(c)],
             arrived.at[step - 1, :, piece_of(c)],
-            grad_send.at[step - 1, c],
+            grad_send,
             grad_recv.at[step - 1, c],
             "ep",
             own_of(step),
@@ -244,12 +266,7 @@
         return carry
 
     lax.fori_loop(0, cuts, start_pairs, 0)
-
-    def start_own(c, carry):
-        pair_copy(0, c).start()
-        return carry
-
-    lax.fori_loop(0, cuts, start_own, 0)
+    own_copy.start()
 
     def send_piece(c, carry):
         for step in order[:-1]:
@@ -259,54 +276,76 @@
                 cols = cols_of(c, i)
                 total = weighted(1, step, cols).astype(jnp.float32)
                 total = total + taken[step, :, cols].astype(jnp.float32)
-                outgoing[step - 1, :, cols] = total.astype(jnp.bfloat16)
+                outgoing[step - 1, :, cols] = coded(total)
                 return inner
 
             lax.fori_loop(0, cut // narrow, add, 0)
             grad_copy(step, c).start()
         return carry
 
-    lax.fori_loop(0, cuts, send_piece, 0)
-
-    @pl.when(z > 0)
+    @pl.when(core == 0)
     def _():
-        pl.semaphore_wait(chain.at[0], 1)
-
-    @pl.when(z < depth - 1)
+        lax.fori_loop(0, cuts, send_piece, 0)
+
+    def pass_up():
+        @pl.when(z > 0)
+        def _():
+            pl.semaphore_wait(chain.at[0], 1)
+
+        @pl.when(z < depth - 1)
+        def _():
+            signal(chain.at[0], "fs", me + across)
+
+    def pass_down():
+        @pl.when(z < depth - 1)
+        def _():
+            pl.semaphore_wait(chain.at[1], 1)
+
+        @pl.when(z > 0)
+        def _():
+            signal(chain.at[1], "fs", me - across)
+
+    @pl.when(z < depth // 2)
     def _():
-        signal(chain.at[0], "fs", me + across)
-        pl.semaphore_wait(chain.at[1], 1)
-
-    @pl.when(z > 0)
+        pass_up()
+        pass_down()
+
+    @pl.when(z >= depth // 2)
     def _():
-        signal(chain.at[1], "fs", me - across)
-
-    def gather_own(c, carry):
-        pair_copy(0, c).wait_recv()
-
-        def one(i, inner):
-            cols = cols_of(c, i)
-            gradient[:, cols] = weighted(1, 0, cols).astype(jnp.float32) + taken[
-                0, :, cols
-            ].astype(jnp.float32)
-            return inner
-
-        return lax.fori_loop(0, cut // narrow, one, carry)
-
-    lax.fori_loop(0, cuts, gather_own, 0)
+        pass_down()
+        pass_up()
+
+    own_copy.wait_recv()
+
+    def gather_own(i, carry):
+        cols = pl.ds(pl.multiple_of(i * narrow, narrow), narrow)
+        mine = weighted(1, 0, cols).astype(jnp.float32)
+        gradient[:, cols] = mine + taken[0, :, cols].astype(jnp.float32)
+        return carry
+
+    lax.fori_loop(0, columns // narrow, gather_own, 0)
     for copy in params:
         copy.wait()
+
+    @pl.when(core > 0)
+    def _():
+        pl.semaphore_wait(go, 1)
+        lax.fori_loop(0, cuts, send_piece, 0)
 
     def moments(c, carry):
         for step in range(1, planes):
             grad_copy(step, c).wait_recv()
+
+        @pl.when(jnp.logical_and(core == 0, c == max(cuts - GO_EARLY, 0)))
+        def _():
+            signal(go, "ep", partner)
 
         def one(i, inner):
             grad_acc, mom_acc = inner
             cols = cols_of(c, i)
             total = gradient[:, cols]
             for step in range(1, planes):
-                total = total + arrived[step - 1, :, cols].astype(jnp.float32)
+                total = total + decoded(arrived[step - 1, :, cols])
             mom_next = MOMENTUM_DECAY * mom[:, cols] + (1.0 - MOMENTUM_DECAY) * total
             gradient[:, cols] = total
             mom[:, cols] = mom_next
@@ -326,28 +365,13 @@
 
     sums[me, 0:1, :] = to_lanes(grad_acc)
     sums[me, 1:2, :] = to_lanes(mom_acc)
-    sum_sends = []
     for step in range(1, shards):
-        copy = remote(
-            sums.at[me],
-            sums.at[me],
-            sum_send.at[step - 1],
-            sum_recv.at[me],
-            "fs",
-            (me + step) % shards,
-        )
-        copy.start()
-        sum_sends.append(copy)
-    for step in range(1, shards):
-        source = (me + step) % shards
         remote(
-            sums.at[source],
-            sums.at[source],
-            sum_send.at[step - 1],
-            sum_recv.at[source],
-            "fs",
-            source,
-        ).wait_recv()
+            sums.at[me], sums.at[me], sum_sem.at[0], sum_sem.at[1], "fs", (me + step) % shards
+        ).start()
+    others = sums.at[pl.ds(0, shards - 1)]
+    all_sums = remote(others, others, sum_sem.at[0], sum_sem.at[1], "fs", (me + 1) % shards)
+    all_sums.wait_recv()
 
     entries = rows * columns * shards
     totals = sums[0]
@@ -412,26 +436,40 @@
     def block(source, k):
         return gathered.at[rows_of(source), pl.ds(pl.multiple_of(k * width, width), width)]
 
-    def send(tree, source, k, which):
+    def far_sem(tree, source, k):
+        if trees[tree][1][1] == 2:
+            k = 0
+        elif not tree:
+            k = k // period
+        return (turned_recv, straight_recv)[tree].at[source, k]
+
+    def send(tree, source, place, k, which):
         for number in which:
             offset, possible = ways[number]
+            near = number in trees[tree][0][3]
 
             @pl.when(possible)
-            def _(number=number, offset=offset):
+            def _(number=number, offset=offset, near=near):
                 piece = block(source, k)
                 remote(
                     piece,
                     piece,
-                    row_send.at[tree, number, source],
-                    row_recv.at[source, k],
+                    row_send.at[tree, number],
+                    near_recv.at[place, k] if near else far_sem(tree, source, k),
                     "fs",
                     me + offset,
                 ).start()
 
-    def await_block(source, k):
+    def await_near(source, place, k):
         piece = block(source, k)
         remote(
-            piece, piece, row_send.at[0, 0, source], row_recv.at[source, k], "fs", source
+            piece, piece, row_send.at[0, 0], near_recv.at[place, k], "fs", source
+        ).wait_recv()
+
+    def await_far(tree, source, k):
+        piece = block(source, k)
+        remote(
+            piece, piece, row_send.at[0, 0], far_sem(tree, source, k), "fs", source
         ).wait_recv()
 
     def live(tree, k):
@@ -453,14 +491,14 @@
                 @pl.when(at >= d)
                 def _():
                     source = me - d * stride
-                    await_block(source, k)
-                    send(tree, source, k, (up,) + second[3])
+                    await_near(source, at - d, k)
+                    send(tree, source, at - d, k, (up,) + second[3])
 
                 @pl.when(at + d < size)
                 def _():
                     source = me + d * stride
-                    await_block(source, k)
-                    send(tree, source, k, (down,) + second[3])
+                    await_near(source, at + d, k)
+                    send(tree, source, at + d, k, (down,) + second[3])
 
         for e in range(length - 2, 0, -1):
             k = t - lag * (size - 1) - LAG * e
@@ -472,14 +510,14 @@
                     @pl.when(jnp.logical_and(other >= e, other < length - 1))
                     def _(level=level):
                         source = level * stride + (other - e) * pitch
-                        await_block(source, k)
-                        send(tree, source, k, (up_other,))
+                        await_far(tree, source, k)
+                        send(tree, source, level, k, (up_other,))
 
                     @pl.when(jnp.logical_and(other + e < length, other > 0))
                     def _(level=level):
                         source = level * stride + (other + e) * pitch
-                        await_block(source, k)
-                        send(tree, source, k, (down_other,))
+                        await_far(tree, source, k)
+                        send(tree, source, level, k, (down_other,))
 
     def turn(t, carry):
         @pl.when(t < chunks)
@@ -495,7 +533,7 @@
 
             @pl.when(live(tree, t))
             def _(tree=tree):
-                send(tree, me, t, (0, 1, 2, 3))
+                send(tree, me, trees[tree][0][0], t, (0, 1, 2, 3))
 
         for tree in (1, 0):
             relay(t, tree)
@@ -512,9 +550,11 @@
             first, second, count = trees[tree]
             _, size, stride, _ = first
             other, length, pitch, _ = second
+            if length == 2:
+                continue
 
             @pl.when(in_tree(tree, k))
-            def _(size=size, stride=stride, other=other, length=length, pitch=pitch):
+            def _(tree=tree, size=size, stride=stride, other=other, length=length, pitch=pitch):
                 for level in range(size):
                     for place in range(length):
                         below = jnp.logical_and(place < other, other == length - 1)
@@ -522,63 +562,60 @@
 
                         @pl.when(jnp.logical_or(below, above))
                         def _(level=level, place=place):
-                            await_block(level * stride + place * pitch, k)
+                            await_far(tree, level * stride + place * pitch, k)
 
         return carry
 
     lax.fori_loop(0, chunks, finish, 0)
-
-    def drain(c, carry):
-        for step in range(planes):
-            pair_copy(step, c).wait_send()
-        for step in range(1, planes):
-            grad_copy(step, c).wait_send()
-        return carry
-
-    lax.fori_loop(0, cuts, drain, 0)
-    for copy in sum_sends:
-        copy.wait_send()
     for tree in range(2):
-        first, _, count = trees[tree]
+        (at, size, stride, moves), (other, length, pitch, far_moves), count = trees[tree]
         if not count:
             continue
-        for number, (_, possible) in enumerate(ways):
-            for source in range(shards):
-                level, place = source // across, source % across
-                used = (level <= z, level >= z, place <= x, place >= x)[number]
-                if first is along_z and number < 2:
-                    used = jnp.logical_and(used, place == x)
-                if first is along_x and number >= 2:
-                    used = jnp.logical_and(used, level == z)
-
-                @pl.when(jnp.logical_and(possible, used))
-                def _(tree=tree, number=number, source=source, count=count):
-                    piece = gathered.at[rows_of(source), pl.ds(0, count * width)]
+        span = pl.ds(0, count * width)
+        if length == 2:
+            for level in range(size):
+                source = level * stride + (1 - other) * pitch
+                piece = gathered.at[rows_of(source), span]
+                remote(
+                    piece, piece, row_send.at[0, 0], far_sem(tree, source, 0), "fs", source
+                ).wait_recv()
+
+        def drain(number, position, extent, going_up, each):
+            for p in range(extent - 1):
+                here = p if going_up else extent - 1 - p
+
+                @pl.when(position == here)
+                def _(p=p):
+                    piece = gathered.at[pl.ds(0, (p + 1) * each * rows), span]
                     remote(
                         piece,
                         piece,
-                        row_send.at[tree, number, source],
-                        row_recv.at[source, 0],
+                        row_send.at[tree, number],
+                        sum_sem.at[1],
                         "fs",
                         (me + 1) % shards,
                     ).wait_send()
 
+        for number, going_up in zip(moves, (True, False)):
+            drain(number, at, size, going_up, 1)
+        for number, going_up in zip(far_moves, (True, False)):
+            drain(number, other, length, going_up, size)
+
+    whole = remote(handed, taken, pair_send, own_recv, "ep", partner)
+    whole.wait_send()
+    remote(outgoing, arrived, grad_send, own_recv, "ep", partner).wait_send()
+    all_sums.wait_send()
+
 
 def flush(gathered, mom, second, gathered_hbm, mom_hbm, second_hbm, sem):
-    copies = []
-    for i, (src, dst) in enumerate(
-        ((gathered, gathered_hbm), (mom, mom_hbm), (second, second_hbm))
-    ):
+    pairs = ((gathered, gathered_hbm), (mom, mom_hbm), (second, second_hbm))
+    for i, (src, dst) in enumerate(pairs):
         height = src.shape[0] // largest_divisor(src.shape[0] // 16, 8)
         for n in range(src.shape[0] // height):
             rows = pl.ds(n * height, height)
-            copies.append(
-                pltpu.make_async_copy(src.at[rows], dst.at[0, rows], sem.at[len(copies)])
-            )
-    for copy in copies:
-        copy.start()
-    for copy in copies:
-        copy.wait()
+            pltpu.make_async_copy(src.at[rows], dst.at[0, rows], sem.at[i]).start()
+    for i, (src, dst) in enumerate(pairs):
+        pltpu.make_async_copy(src, dst.at[0], sem.at[i]).wait()
 
 
 def per_device(
@@ -590,6 +627,7 @@
     planes = groups // CORES
     chunks = largest_divisor(columns // LANES, MOST_CHUNKS)
     cuts = largest_divisor(columns // LANES, MOST_CUTS)
+    turned = turned_chunks(depth, across, chunks)
     hbm = pl.BlockSpec(memory_space=pltpu.HBM)
     vmem = pl.BlockSpec(memory_space=pltpu.VMEM)
     held = (2 * shards + 8) * rows * columns
@@ -618,17 +656,20 @@
             pltpu.VMEM((shards, 2, LANES), jnp.float32),
             pltpu.SMEM((in_bias.shape[0],), jnp.float32),
             pltpu.SemaphoreType.DMA((5,)),
-            pltpu.SemaphoreType.DMA((CORES, planes)),
+            pltpu.SemaphoreType.DMA((CORES,)),
             pltpu.SemaphoreType.DMA((3,)),
-            pltpu.SemaphoreType.DMA((planes, cuts)),
-            pltpu.SemaphoreType.DMA((planes, cuts)),
+            pltpu.SemaphoreType.DMA,
             pltpu.SemaphoreType.DMA((planes - 1, cuts)),
+            pltpu.SemaphoreType.DMA,
+            pltpu.SemaphoreType.DMA,
             pltpu.SemaphoreType.DMA((planes - 1, cuts)),
             pltpu.SemaphoreType.REGULAR((2,)),
-            pltpu.SemaphoreType.DMA((shards - 1,)),
-            pltpu.SemaphoreType.DMA((shards,)),
-            pltpu.SemaphoreType.DMA((2, 4, shards)),
-            pltpu.SemaphoreType.DMA((shards, chunks)),
+            pltpu.SemaphoreType.REGULAR,
+            pltpu.SemaphoreType.DMA((2,)),
+            pltpu.SemaphoreType.DMA((2, 4)),
+            pltpu.SemaphoreType.DMA((max(depth, across), chunks)),
+            pltpu.SemaphoreType.DMA((shards, 1 if depth == 2 else max(turned, 1))),
+            pltpu.SemaphoreType.DMA((shards, 1 if across == 2 else chunks)),
         ],
         compiler_params=pltpu.CompilerParams(
             collective_id=0,
@@ -646,7 +687,7 @@
         ),
         in_specs=[vmem] * 3,
         out_specs=(hbm, hbm, hbm),
-        scratch_shapes=[pltpu.SemaphoreType.DMA((24,))],
+        scratch_shapes=[pltpu.SemaphoreType.DMA((3,))],
         compiler_params=pltpu.CompilerParams(
             has_side_effects=True, vmem_limit_bytes=FLUSH_BYTES
         ),

time: 71.7 us -> 64.5 us (0.90)
  the two profiles are of different devices: /device:TPU:0 before, /device:TPU:1 now
where the time goes in v2:
time: 64.5 us; the launch traced here: 64.3 us
  Pallas kernels  63.7 us (99%)
    pallas_call x1, Pallas kernels, per_device(): pl.pallas_call(functools.partial(kernel, groups, depth, across, chunks),...  61.2 us
    pallas_call x1, Pallas kernels, per_device(): pl.pallas_call(flush, out_shape=(jax.ShapeDtypeStruct((1, rows * shards,...  2.46 us

profile of v2, /device:TPU:1, one launch (start us, length us, event | category | flops | bytes accessed | tf_op | source)
XLA Modules:
  0.0 64.3 jit_solution(5487119103534412134)
XLA Ops:
  0.6 61.2 %learned_update.1 = (bf16[128,14336]{1,0:T(8,128)(2,1)S(1)}, f32[16,14336]{1,0:T(8,128)S(1)}, f32[16,14336]{1,0:T(8,128)S(1)}) custom-call(s32[4,4]{1,0:T(4,128)} %counts_hbm.1, f32[6,32]{1,0:T(8,128)} %in_weight_hbm.1, f32[32]{0:T(128)} %in_bias_hbm.1, f32[2,32]{1,0:T(2,128)} %bitcast.1, f32[2]{0:T(128)} %out_bias_hbm.1, ...), custom_call_target="tpu_custom_call" | custom-call | tf_op jit(solution)/shard_map/learned_update/pallas_call | solution.py:634
  61.8 2.5 %flush.1 = (bf16[1,128,14336]{2,1,0:T(8,128)(2,1)}, f32[1,16,14336]{2,1,0:T(8,128)}, f32[1,16,14336]{2,1,0:T(8,128)}) custom-call(bf16[128,14336]{1,0:T(8,128)(2,1)S(1)} %get-tuple-element.6.gathered, f32[16,14336]{1,0:T(8,128)S(1)} %get-tuple-element.7.mom, f32[16,14336]{1,0:T(8,128)S(1)} %get-tuple-element.8.second), custom_call_target="tpu_custom_call" | custom-call | tf_op jit(solution)/shard_map/flush/pallas_call | solution.py:681

commit v3 on v2

--- a/solution.py
+++ b/solution.py
@@ -20,10 +20,12 @@
 CODE_SCALE = 512.0
 CODE_LEAST = 2.0**-126
 GO_EARLY = 3
-LAG = 3
+LAG = 2
 TURN_LAG = 3
 VMEM_BYTES = 67043328
 FLUSH_BYTES = 1 << 20
+TERMS = 16
+MOST_TILE = 1024
 
 
 def largest_divisor(number, most):
@@ -105,7 +107,8 @@
     arrived,
     gradient,
     sums,
-    bias,
+    layer,
+    floor,
     small_sem,
     slab_sem,
     param_sem,
@@ -327,6 +330,28 @@
     for copy in params:
         copy.wait()
 
+    span = layer.shape[1]
+    lane = lax.broadcasted_iota(jnp.int32, (rows, span), 1)
+    term = lane // rows
+    inside = lane % rows == lax.broadcasted_iota(jnp.int32, (rows, span), 0)
+
+    def lay(h, carry):
+        high = jnp.zeros((rows, span), jnp.float32)
+        low = high
+        for f in range(5):
+            value = jnp.full((rows, span), in_weight[f, h])
+            upper = value.astype(jnp.bfloat16).astype(jnp.float32)
+            at_high = term == f
+            if f < 4:
+                at_high = jnp.logical_or(at_high, term == 5 + f)
+            high = jnp.where(at_high, upper, high)
+            low = jnp.where(term == 9 + f, value - upper, low)
+        block = jnp.where(inside, high + low, 0.0)
+        layer[pl.ds(pl.multiple_of(h * rows, rows), rows), :] = block.astype(jnp.bfloat16)
+        return carry
+
+    lax.fori_loop(0, units, lay, 0)
+
     @pl.when(core > 0)
     def _():
         pl.semaphore_wait(go, 1)
@@ -382,35 +407,45 @@
     inv_grad = inverse[0:1, :1]
     inv_mom = inverse[1:2, :1]
     log_mom = jnp.max(0.5 * jnp.log(mean[1:2, :]))
+    starts = [out_bias[0], out_bias[1]]
     for h in range(units):
-        bias[h] = in_bias[h] + in_weight[5, h] * log_mom
+        bias = in_bias[h] + in_weight[5, h] * log_mom
+        floor[h] = -bias
+        for i in range(2):
+            starts[i] = starts[i] + bias * out_weight[i, h]
 
     width = columns // chunks
-    tile = tile_width(width, 256)
+    tile = tile_width(width, MOST_TILE)
 
     def learned_step(cols):
         grad = gradient[:, cols]
         mom_next = mom[:, cols]
-        old = weight[:, cols].astype(jnp.float32)
+        old = weight[:, cols]
         inv_root = lax.rsqrt(second[:, cols] + ROOT_EPS)
         features = (
             grad * inv_grad,
             mom_next * inv_mom,
             mom_next * inv_root,
             grad * inv_root,
-            old,
         )
-        direction = jnp.full(grad.shape, out_bias[0])
-        magnitude = jnp.full(grad.shape, out_bias[1])
+        high = [feature.astype(jnp.bfloat16) for feature in features]
+        low = [
+            (feature - part.astype(jnp.float32)).astype(jnp.bfloat16)
+            for feature, part in zip(features, high)
+        ]
+        terms = [*high, old, *low, *high, old]
+        terms = terms + [jnp.zeros_like(old)] * (TERMS - len(terms))
+        hidden = jnp.dot(
+            layer[...], jnp.concatenate(terms, axis=0), preferred_element_type=jnp.float32
+        )
+        direction = jnp.full(grad.shape, starts[0])
+        magnitude = jnp.full(grad.shape, starts[1])
         for h in range(units):
-            hidden = features[0] * in_weight[0, h] + bias[h]
-            for f in range(1, len(features)):
-                hidden = hidden + features[f] * in_weight[f, h]
-            hidden = jnp.maximum(hidden, 0.0)
-            direction = direction + hidden * out_weight[0, h]
-            magnitude = magnitude + hidden * out_weight[1, h]
+            above = jnp.maximum(hidden[h * rows : (h + 1) * rows], floor[h])
+            direction = direction + above * out_weight[0, h]
+            magnitude = magnitude + above * out_weight[1, h]
         update = STEP_SCALE * direction * jnp.exp(EXP_SCALE * magnitude)
-        return (old - update).astype(jnp.bfloat16)
+        return (old.astype(jnp.float32) - update).astype(jnp.bfloat16)
 
     def rows_of(source):
         return pl.ds(pl.multiple_of(source * rows, rows), rows)
@@ -654,6 +689,7 @@
             pltpu.VMEM((planes - 1, rows, columns), jnp.bfloat16),
             pltpu.VMEM((rows, columns), jnp.float32),
             pltpu.VMEM((shards, 2, LANES), jnp.float32),
+            pltpu.VMEM((in_bias.shape[0] * rows, TERMS * rows), jnp.bfloat16),
             pltpu.SMEM((in_bias.shape[0],), jnp.float32),
             pltpu.SemaphoreType.DMA((5,)),
             pltpu.SemaphoreType.DMA((CORES,)),

time: 64.5 us -> 62.4 us (0.967)
  the two profiles are of different devices: /device:TPU:1 before, /device:TPU:0 now
where the time goes in v3:
time: 62.4 us; the launch traced here: 61.7 us
  Pallas kernels  61 us (98%)
  between operations  0.64 us (1%)
    pallas_call x1, Pallas kernels, per_device(): pl.pallas_call(functools.partial(kernel, groups, depth, across, chunks),...  58.6 us
    pallas_call x1, Pallas kernels, per_device(): pl.pallas_call(flush, out_shape=(jax.ShapeDtypeStruct((1, rows * shards,...  2.46 us

profile of v3, /device:TPU:0, one launch (start us, length us, event | category | flops | bytes accessed | tf_op | source)
XLA Modules:
  0.0 61.7 jit_solution(13191161887915120824)
XLA Ops:
  0.6 58.6 %learned_update.1 = (bf16[128,14336]{1,0:T(8,128)(2,1)S(1)}, f32[16,14336]{1,0:T(8,128)S(1)}, f32[16,14336]{1,0:T(8,128)S(1)}) custom-call(s32[4,4]{1,0:T(4,128)} %counts_hbm.1, f32[6,32]{1,0:T(8,128)} %in_weight_hbm.1, f32[32]{0:T(128)} %in_bias_hbm.1, f32[2,32]{1,0:T(2,128)} %bitcast.1, f32[2]{0:T(128)} %out_bias_hbm.1, ...), custom_call_target="tpu_custom_call" | custom-call | tf_op jit(solution)/shard_map/learned_update/pallas_call | solution.py:669
  59.2 2.5 %flush.1 = (bf16[1,128,14336]{2,1,0:T(8,128)(2,1)}, f32[1,16,14336]{2,1,0:T(8,128)}, f32[1,16,14336]{2,1,0:T(8,128)}) custom-call(bf16[128,14336]{1,0:T(8,128)(2,1)S(1)} %get-tuple-element.6.gathered, f32[16,14336]{1,0:T(8,128)S(1)} %get-tuple-element.7.mom, f32[16,14336]{1,0:T(8,128)S(1)} %get-tuple-element.8.second), custom_call_target="tpu_custom_call" | custom-call | tf_op jit(solution)/shard_map/flush/pallas_call | solution.py:717

commit v4 on v3

--- a/solution.py
+++ b/solution.py
@@ -14,14 +14,16 @@
 STEP_SCALE = 0.2
 EXP_SCALE = 0.5
 LANES = 128
+SUBLANES = 8
 CORES = 2
 MOST_CHUNKS = 14
 MOST_CUTS = 7
 CODE_SCALE = 512.0
 CODE_LEAST = 2.0**-126
 GO_EARLY = 3
-LAG = 2
-TURN_LAG = 3
+NEAR_LAGS = (4, 8, 10)
+TURN_LAG = 8
+FAR_LAGS = (6, 10)
 VMEM_BYTES = 67043328
 FLUSH_BYTES = 1 << 20
 TERMS = 16
@@ -44,6 +46,10 @@
         return max(on_x, on_z)
 
     return min(range(chunks + 1), key=load)
+
+
+def nth(lags, d):
+    return lags[d - 1] if d <= len(lags) else lags[-1] * d
 
 
 def remote(src, dst, send_sem, recv_sem, axis, peer):
@@ -69,6 +75,18 @@
     fourth = lax.rsqrt(lax.rsqrt(jnp.maximum(jnp.abs(code), CODE_LEAST)))
     size = fourth * lax.rsqrt(fourth) * (1.0 / CODE_SCALE)
     return jnp.where(code == 0.0, 0.0, jnp.where(code < 0.0, -size, size))
+
+
+def folded(value):
+    rows, columns = value.shape
+    parts = [
+        value[i : i + SUBLANES, j : j + LANES]
+        for i in range(0, rows, SUBLANES)
+        for j in range(0, columns, LANES)
+    ]
+    while len(parts) > 1:
+        parts = [a + b for a, b in zip(parts[::2], parts[1::2])] + parts[len(parts) & ~1 :]
+    return parts[0]
 
 
 def signal(semaphore, axis, peer):
@@ -108,7 +126,6 @@
     gradient,
     sums,
     layer,
-    floor,
     small_sem,
     slab_sem,
     param_sem,
@@ -170,21 +187,22 @@
             )
         )
     ]
-    for copy in small:
-        copy.start()
-
-    order = [*range(1, planes), 0]
-    for kind, expert_of in enumerate((other_of, own_of)):
-        for step in order:
-            pltpu.make_async_copy(
-                grads_hbm.at[0, expert_of(step)], grads.at[kind, step], slab_sem.at[kind]
-            ).start()
+    def start_slab(kind, step):
+        expert = (other_of, own_of)[kind](step)
+        sem = slab_sem.at[kind if step else CORES]
+        pltpu.make_async_copy(grads_hbm.at[0, expert], grads.at[kind, step], sem).start()
 
     def await_slabs(kind):
         pltpu.make_async_copy(
-            grads_hbm.at[0, pl.ds(0, planes)], grads.at[kind], slab_sem.at[kind]
+            grads_hbm.at[0, pl.ds(0, planes - 1)],
+            grads.at[kind, pl.ds(1, planes - 1)],
+            slab_sem.at[kind],
         ).wait()
 
+    small[0].start()
+    for kind in range(CORES):
+        for step in range(1, planes):
+            start_slab(kind, step)
     params = [
         pltpu.make_async_copy(src.at[0], dst, param_sem.at[i])
         for i, (src, dst) in enumerate(
@@ -195,8 +213,6 @@
             )
         )
     ]
-    for copy in params:
-        copy.start()
 
     cuts = grad_recv.shape[1]
     cut = columns // cuts
@@ -208,8 +224,7 @@
     def piece_of(c):
         return pl.ds(pl.multiple_of(c * cut, cut), cut)
 
-    for copy in small:
-        copy.wait()
+    small[0].wait()
 
     def share_of(expert):
         total = counts[0, expert]
@@ -225,17 +240,6 @@
     def weighted(kind, step, cols):
         value = shares[kind][step] * grads[kind, step, :, cols].astype(jnp.float32)
         return value.astype(jnp.bfloat16)
-
-    await_slabs(0)
-
-    def hand(i, carry):
-        cols = pl.ds(pl.multiple_of(i * narrow, narrow), narrow)
-        for step in order:
-            handed[step, :, cols] = weighted(0, step, cols)
-        return carry
-
-    lax.fori_loop(0, columns // narrow, hand, 0)
-    await_slabs(1)
 
     near = 1 + (planes - 1) + (across - 1)
     near = near + (z > 0).astype(jnp.int32) + (z < depth - 1).astype(jnp.int32)
@@ -264,15 +268,27 @@
         )
 
     def start_pairs(c, carry):
-        for step in order[:-1]:
+        for step in range(1, planes):
+
+            def hand(i, inner, step=step):
+                cols = cols_of(c, i)
+                handed[step, :, cols] = weighted(0, step, cols)
+                return inner
+
+            lax.fori_loop(0, cut // narrow, hand, 0)
             pair_copy(step, c).start()
         return carry
 
+    await_slabs(0)
     lax.fori_loop(0, cuts, start_pairs, 0)
-    own_copy.start()
+    for kind in range(CORES):
+        start_slab(kind, 0)
+    for copy in params + small[1:]:
+        copy.start()
+    await_slabs(1)
 
     def send_piece(c, carry):
-        for step in order[:-1]:
+        for step in range(1, planes):
             pair_copy(step, c).wait_recv()
 
             def add(i, inner, step=step):
@@ -286,7 +302,7 @@
             grad_copy(step, c).start()
         return carry
 
-    @pl.when(core == 0)
+    @pl.when(core > 0)
     def _():
         lax.fori_loop(0, cuts, send_piece, 0)
 
@@ -318,6 +334,19 @@
         pass_down()
         pass_up()
 
+    pltpu.make_async_copy(
+        grads_hbm.at[0, pl.ds(0, CORES)], grads.at[:, 0], slab_sem.at[CORES]
+    ).wait()
+
+    def hand_own(i, carry):
+        cols = pl.ds(pl.multiple_of(i * narrow, narrow), narrow)
+        handed[0, :, cols] = weighted(0, 0, cols)
+        return carry
+
+    lax.fori_loop(0, columns // narrow, hand_own, 0)
+    own_copy.start()
+    for copy in small[1:]:
+        copy.wait()
     own_copy.wait_recv()
 
     def gather_own(i, carry):
@@ -351,8 +380,17 @@
         return carry
 
     lax.fori_loop(0, units, lay, 0)
-
-    @pl.when(core > 0)
+    starts = []
+    slopes = []
+    for i in range(2):
+        start, slope = out_bias[i], 0.0
+        for h in range(units):
+            start = start + in_bias[h] * out_weight[i, h]
+            slope = slope + in_weight[5, h] * out_weight[i, h]
+        starts.append(start)
+        slopes.append(slope)
+
+    @pl.when(core == 0)
     def _():
         pl.semaphore_wait(go, 1)
         lax.fori_loop(0, cuts, send_piece, 0)
@@ -361,7 +399,7 @@
         for step in range(1, planes):
             grad_copy(step, c).wait_recv()
 
-        @pl.when(jnp.logical_and(core == 0, c == max(cuts - GO_EARLY, 0)))
+        @pl.when(jnp.logical_and(core > 0, c == max(cuts - GO_EARLY, 0)))
         def _():
             signal(go, "ep", partner)
 
@@ -377,19 +415,14 @@
             second[:, cols] = (
                 SECOND_DECAY * second[:, cols] + (1.0 - SECOND_DECAY) * total * total
             )
-            return grad_acc + total * total, mom_acc + mom_next * mom_next
+            return grad_acc + folded(total * total), mom_acc + folded(mom_next * mom_next)
 
         return lax.fori_loop(0, cut // narrow, one, carry)
 
-    zero = jnp.zeros((rows, narrow), jnp.float32)
+    zero = jnp.zeros((SUBLANES, LANES), jnp.float32)
     grad_acc, mom_acc = lax.fori_loop(0, cuts, moments, (zero, zero))
-
-    def to_lanes(acc):
-        acc = jnp.sum(acc, axis=0, keepdims=True)
-        return sum(acc[:, j : j + LANES] for j in range(0, narrow, LANES))
-
-    sums[me, 0:1, :] = to_lanes(grad_acc)
-    sums[me, 1:2, :] = to_lanes(mom_acc)
+    sums[me, 0] = grad_acc
+    sums[me, 1] = mom_acc
     for step in range(1, shards):
         remote(
             sums.at[me], sums.at[me], sum_sem.at[0], sum_sem.at[1], "fs", (me + step) % shards
@@ -402,17 +435,11 @@
     totals = sums[0]
     for s in range(1, shards):
         totals = totals + sums[s]
-    mean = jnp.broadcast_to(jnp.sum(totals, axis=1, keepdims=True) / entries, (2, LANES)) + NORM_EPS
+    mean = jnp.sum(totals, axis=(1, 2), keepdims=True) / entries + NORM_EPS
     inverse = lax.rsqrt(mean)
-    inv_grad = inverse[0:1, :1]
-    inv_mom = inverse[1:2, :1]
-    log_mom = jnp.max(0.5 * jnp.log(mean[1:2, :]))
-    starts = [out_bias[0], out_bias[1]]
-    for h in range(units):
-        bias = in_bias[h] + in_weight[5, h] * log_mom
-        floor[h] = -bias
-        for i in range(2):
-            starts[i] = starts[i] + bias * out_weight[i, h]
+    inv_grad = inverse[0]
+    inv_mom = inverse[1]
+    log_mom = 0.5 * jnp.log(mean[1])
 
     width = columns // chunks
     tile = tile_width(width, MOST_TILE)
@@ -438,10 +465,13 @@
         hidden = jnp.dot(
             layer[...], jnp.concatenate(terms, axis=0), preferred_element_type=jnp.float32
         )
-        direction = jnp.full(grad.shape, starts[0])
-        magnitude = jnp.full(grad.shape, starts[1])
+        direction, magnitude = (
+            jnp.broadcast_to(start + slope * log_mom, grad.shape)
+            for start, slope in zip(starts, slopes)
+        )
         for h in range(units):
-            above = jnp.maximum(hidden[h * rows : (h + 1) * rows], floor[h])
+            floor = -in_bias[h] - in_weight[5, h] * log_mom
+            above = jnp.maximum(hidden[h * rows : (h + 1) * rows], floor)
             direction = direction + above * out_weight[0, h]
             magnitude = magnitude + above * out_weight[1, h]
         update = STEP_SCALE * direction * jnp.exp(EXP_SCALE * magnitude)
@@ -465,7 +495,8 @@
     def in_tree(tree, k):
         if not turned:
             return k >= 0 if tree else k < 0
-        chosen = jnp.logical_and(k % period == period // 2, k // period < turned)
+        low = (chunks - turned) // 2
+        chosen = jnp.logical_and(k >= low, k < low + turned)
         return jnp.logical_not(chosen) if tree else chosen
 
     def block(source, k):
@@ -475,7 +506,7 @@
         if trees[tree][1][1] == 2:
             k = 0
         elif not tree:
-            k = k // period
+            k = k - (chunks - turned) // 2
         return (turned_recv, straight_recv)[tree].at[source, k]
 
     def send(tree, source, place, k, which):
@@ -490,7 +521,7 @@
                     piece,
                     piece,
                     row_send.at[tree, number],
-                    near_recv.at[place, k] if near else far_sem(tree, source, k),
+                    near_recv.at[place - number % 2, k] if near else far_sem(tree, source, k),
                     "fs",
                     me + offset,
                 ).start()
@@ -510,6 +541,9 @@
     def live(tree, k):
         inside = jnp.logical_and(k >= 0, k < chunks)
         return jnp.logical_and(inside, in_tree(tree, jnp.maximum(k, 0)))
+
+    def near_lag(tree, d):
+        return nth(NEAR_LAGS, d) if tree else TURN_LAG * d
 
     def relay(t, tree):
         first, second, count = trees[tree]
@@ -517,9 +551,8 @@
             return
         at, size, stride, (up, down) = first
         other, length, pitch, (up_other, down_other) = second
-        lag = LAG if tree else TURN_LAG
         for d in range(size - 1, 0, -1):
-            k = t - lag * d
+            k = t - near_lag(tree, d)
 
             @pl.when(live(tree, k))
             def _(d=d, k=k):
@@ -532,11 +565,11 @@
                 @pl.when(at + d < size)
                 def _():
                     source = me + d * stride
-                    await_near(source, at + d, k)
+                    await_near(source, at + d - 1, k)
                     send(tree, source, at + d, k, (down,) + second[3])
 
         for e in range(length - 2, 0, -1):
-            k = t - lag * (size - 1) - LAG * e
+            k = t - near_lag(tree, size - 1) - nth(FAR_LAGS, e)
 
             @pl.when(live(tree, k))
             def _(e=e, k=k):
@@ -575,8 +608,9 @@
         return carry
 
     reach = max(
-        LAG * (depth - 1) + LAG * max(across - 2, 0),
-        TURN_LAG * (across - 1) + LAG * max(depth - 2, 0),
+        near_lag(tree, first[1] - 1) + (nth(FAR_LAGS, second[1] - 2) if second[1] > 2 else 0)
+        for tree, (first, second, count) in enumerate(trees)
+        if count
     )
     lax.fori_loop(0, chunks + reach, turn, 0)
 
@@ -688,11 +722,10 @@
             pltpu.VMEM((planes - 1, rows, columns), jnp.bfloat16),
             pltpu.VMEM((planes - 1, rows, columns), jnp.bfloat16),
             pltpu.VMEM((rows, columns), jnp.float32),
-            pltpu.VMEM((shards, 2, LANES), jnp.float32),
+            pltpu.VMEM((shards, 2, SUBLANES, LANES), jnp.float32),
             pltpu.VMEM((in_bias.shape[0] * rows, TERMS * rows), jnp.bfloat16),
-            pltpu.SMEM((in_bias.shape[0],), jnp.float32),
             pltpu.SemaphoreType.DMA((5,)),
-            pltpu.SemaphoreType.DMA((CORES,)),
+            pltpu.SemaphoreType.DMA((CORES + 1,)),
             pltpu.SemaphoreType.DMA((3,)),
             pltpu.SemaphoreType.DMA,
             pltpu.SemaphoreType.DMA((planes - 1, cuts)),
@@ -703,7 +736,7 @@
             pltpu.SemaphoreType.REGULAR,
             pltpu.SemaphoreType.DMA((2,)),
             pltpu.SemaphoreType.DMA((2, 4)),
-            pltpu.SemaphoreType.DMA((max(depth, across), chunks)),
+            pltpu.SemaphoreType.DMA((max(depth, across) - 1, chunks)),
             pltpu.SemaphoreType.DMA((shards, 1 if depth == 2 else max(turned, 1))),
             pltpu.SemaphoreType.DMA((shards, 1 if across == 2 else chunks)),
         ],

time: 62.4 us -> 60 us (0.962)
  Pallas kernels: 61 us -> 59.2 us
    pallas_call x1, Pallas kernels: 58.6 us -> 56.7 us  [per_device(): pl.pallas_call(functools.partial(kernel, groups, depth, across, chunks),...]
where the time goes in v4:
time: 60 us; the launch traced here: 59.8 us
  Pallas kernels  59.2 us (99%)
  between operations  0.64 us (1%)
    pallas_call x1, Pallas kernels, per_device(): pl.pallas_call(functools.partial(kernel, groups, depth, across, chunks),...  56.7 us
    pallas_call x1, Pallas kernels, per_device(): pl.pallas_call(flush, out_shape=(jax.ShapeDtypeStruct((1, rows * shards,...  2.46 us

profile of v4, /device:TPU:0, one launch (start us, length us, event | category | flops | bytes accessed | tf_op | source)
XLA Modules:
  0.0 59.8 jit_solution(9001410762010213312)
XLA Ops:
  0.6 56.7 %learned_update.1 = (bf16[128,14336]{1,0:T(8,128)(2,1)S(1)}, f32[16,14336]{1,0:T(8,128)S(1)}, f32[16,14336]{1,0:T(8,128)S(1)}) custom-call(s32[4,4]{1,0:T(4,128)} %counts_hbm.1, f32[6,32]{1,0:T(8,128)} %in_weight_hbm.1, f32[32]{0:T(128)} %in_bias_hbm.1, f32[2,32]{1,0:T(2,128)} %bitcast.1, f32[2]{0:T(128)} %out_bias_hbm.1, ...), custom_call_target="tpu_custom_call" | custom-call | tf_op jit(solution)/shard_map/learned_update/pallas_call | solution.py:703
  57.3 2.5 %flush.1 = (bf16[1,128,14336]{2,1,0:T(8,128)(2,1)}, f32[1,16,14336]{2,1,0:T(8,128)}, f32[1,16,14336]{2,1,0:T(8,128)}) custom-call(bf16[128,14336]{1,0:T(8,128)(2,1)S(1)} %get-tuple-element.6.gathered, f32[16,14336]{1,0:T(8,128)S(1)} %get-tuple-element.7.mom, f32[16,14336]{1,0:T(8,128)S(1)} %get-tuple-element.8.second), custom_call_target="tpu_custom_call" | custom-call | tf_op jit(solution)/shard_map/flush/pallas_call | solution.py:750

commit v5 on v4

--- a/solution.py
+++ b/solution.py
@@ -21,9 +21,9 @@
 CODE_SCALE = 512.0
 CODE_LEAST = 2.0**-126
 GO_EARLY = 3
-NEAR_LAGS = (4, 8, 10)
+NEAR_LAGS = (3, 6, 9)
 TURN_LAG = 8
-FAR_LAGS = (6, 10)
+FAR_LAGS = (10, 14)
 VMEM_BYTES = 67043328
 FLUSH_BYTES = 1 << 20
 TERMS = 16
@@ -41,7 +41,7 @@
 def turned_chunks(depth, across, chunks):
     def load(turned):
         straight = chunks - turned
-        on_x = (across - 1) * (depth * straight + turned)
+        on_x = (across - 1) * (depth * straight + (0 if across == 2 else turned))
         on_z = (depth - 1) * (straight + across * turned)
         return max(on_x, on_z)
 
@@ -126,6 +126,7 @@
     gradient,
     sums,
     layer,
+    extra,
     small_sem,
     slab_sem,
     param_sem,
@@ -141,6 +142,8 @@
     near_recv,
     turned_recv,
     straight_recv,
+    extra_send,
+    extra_recv,
 ):
     shards = depth * across
     planes = groups // CORES
@@ -216,6 +219,13 @@
 
     cuts = grad_recv.shape[1]
     cut = columns // cuts
+    width = columns // chunks
+    turned = turned_chunks(depth, across, chunks)
+    low = chunks - turned
+    doubled = across == 2 and turned > 0
+    first_cut = low * width // cut if doubled else 0
+    last_cut = -(-(low + turned) * width // cut) if doubled else 0
+    peer = me + 1 - 2 * x
     narrow = tile_width(cut, 1024)
 
     def cols_of(c, i):
@@ -267,7 +277,8 @@
             own_of(step),
         )
 
-    def start_pairs(c, carry):
+    def start_pairs(n, carry):
+        c = (n + first_cut) % cuts
         for step in range(1, planes):
 
             def hand(i, inner, step=step):
@@ -287,7 +298,8 @@
         copy.start()
     await_slabs(1)
 
-    def send_piece(c, carry):
+    def send_piece(n, carry):
+        c = (n + first_cut) % cuts
         for step in range(1, planes):
             pair_copy(step, c).wait_recv()
 
@@ -358,6 +370,31 @@
     lax.fori_loop(0, columns // narrow, gather_own, 0)
     for copy in params:
         copy.wait()
+
+    def extra_copy(i):
+        return remote(
+            extra.at[0, i], extra.at[1, i], extra_send, extra_recv.at[i // 3], "fs", peer
+        )
+
+    reached = extra.shape[3]
+    bite = tile_width(reached, 1024)
+
+    def spare(i):
+        here = pl.multiple_of(i * bite, bite)
+        return pl.ds(here, bite), pl.ds(pl.multiple_of(low * width + here, LANES), bite)
+
+    if doubled:
+
+        def share_state(i, carry):
+            near_cols, cols = spare(i)
+            extra[0, 0, :, near_cols] = coded(mom[:, cols])
+            extra[0, 1, :, near_cols] = coded(second[:, cols])
+            extra[0, 2, :, near_cols] = weight[:, cols]
+            return carry
+
+        lax.fori_loop(0, reached // bite, share_state, 0)
+        for i in range(3):
+            extra_copy(i).start()
 
     span = layer.shape[1]
     lane = lax.broadcasted_iota(jnp.int32, (rows, span), 1)
@@ -395,11 +432,12 @@
         pl.semaphore_wait(go, 1)
         lax.fori_loop(0, cuts, send_piece, 0)
 
-    def moments(c, carry):
+    def moments(n, carry):
+        c = (n + first_cut) % cuts
         for step in range(1, planes):
             grad_copy(step, c).wait_recv()
 
-        @pl.when(jnp.logical_and(core > 0, c == max(cuts - GO_EARLY, 0)))
+        @pl.when(jnp.logical_and(core > 0, n == max(cuts - GO_EARLY, 0)))
         def _():
             signal(go, "ep", partner)
 
@@ -420,7 +458,17 @@
         return lax.fori_loop(0, cut // narrow, one, carry)
 
     zero = jnp.zeros((SUBLANES, LANES), jnp.float32)
-    grad_acc, mom_acc = lax.fori_loop(0, cuts, moments, (zero, zero))
+    sofar = lax.fori_loop(0, last_cut - first_cut, moments, (zero, zero))
+    if doubled:
+
+        def share_gradient(i, carry):
+            near_cols, cols = spare(i)
+            extra[0, 3, :, near_cols] = coded(gradient[:, cols])
+            return carry
+
+        lax.fori_loop(0, reached // bite, share_gradient, 0)
+        extra_copy(3).start()
+    grad_acc, mom_acc = lax.fori_loop(last_cut - first_cut, cuts, moments, sofar)
     sums[me, 0] = grad_acc
     sums[me, 1] = mom_acc
     for step in range(1, shards):
@@ -441,14 +489,10 @@
     inv_mom = inverse[1]
     log_mom = 0.5 * jnp.log(mean[1])
 
-    width = columns // chunks
     tile = tile_width(width, MOST_TILE)
 
-    def learned_step(cols):
-        grad = gradient[:, cols]
-        mom_next = mom[:, cols]
-        old = weight[:, cols]
-        inv_root = lax.rsqrt(second[:, cols] + ROOT_EPS)
+    def network(grad, mom_next, second_next, old):
+        inv_root = lax.rsqrt(second_next + ROOT_EPS)
         features = (
             grad * inv_grad,
             mom_next * inv_mom,
@@ -477,6 +521,20 @@
         update = STEP_SCALE * direction * jnp.exp(EXP_SCALE * magnitude)
         return (old.astype(jnp.float32) - update).astype(jnp.bfloat16)
 
+    def learned_step(cols):
+        return network(gradient[:, cols], mom[:, cols], second[:, cols], weight[:, cols])
+
+    def doubled_step(slot, cols):
+        mom_before, second_before, grad = (
+            decoded(extra[slot, i, :, cols]) for i in (0, 1, 3)
+        )
+        return network(
+            grad,
+            MOMENTUM_DECAY * mom_before + (1.0 - MOMENTUM_DECAY) * grad,
+            SECOND_DECAY * second_before + (1.0 - SECOND_DECAY) * grad * grad,
+            extra[slot, 2, :, cols],
+        )
+
     def rows_of(source):
         return pl.ds(pl.multiple_of(source * rows, rows), rows)
 
@@ -486,8 +544,6 @@
         (1, x < across - 1),
         (-1, x > 0),
     )
-    turned = turned_chunks(depth, across, chunks)
-    period = chunks // turned if turned else chunks
     along_z = (z, depth, across, (0, 1))
     along_x = (x, across, 1, (2, 3))
     trees = ((along_x, along_z, turned), (along_z, along_x, chunks - turned))
@@ -495,7 +551,7 @@
     def in_tree(tree, k):
         if not turned:
             return k >= 0 if tree else k < 0
-        low = (chunks - turned) // 2
+        low = chunks - turned
         chosen = jnp.logical_and(k >= low, k < low + turned)
         return jnp.logical_not(chosen) if tree else chosen
 
@@ -506,7 +562,7 @@
         if trees[tree][1][1] == 2:
             k = 0
         elif not tree:
-            k = k - (chunks - turned) // 2
+            k = k - (chunks - turned)
         return (turned_recv, straight_recv)[tree].at[source, k]
 
     def send(tree, source, place, k, which):
@@ -543,7 +599,9 @@
         return jnp.logical_and(inside, in_tree(tree, jnp.maximum(k, 0)))
 
     def near_lag(tree, d):
-        return nth(NEAR_LAGS, d) if tree else TURN_LAG * d
+        if tree:
+            return nth(NEAR_LAGS, d)
+        return 0 if doubled else TURN_LAG * d
 
     def relay(t, tree):
         first, second, count = trees[tree]
@@ -551,7 +609,7 @@
             return
         at, size, stride, (up, down) = first
         other, length, pitch, (up_other, down_other) = second
-        for d in range(size - 1, 0, -1):
+        for d in range(0 if doubled and not tree else size - 1, 0, -1):
             k = t - near_lag(tree, d)
 
             @pl.when(live(tree, k))
@@ -588,7 +646,7 @@
                         send(tree, source, level, k, (down_other,))
 
     def turn(t, carry):
-        @pl.when(t < chunks)
+        @pl.when(jnp.logical_and(t < chunks, in_tree(1, t)) if doubled else t < chunks)
         def _():
             def one(i, inner):
                 cols = pl.ds(pl.multiple_of(t * width + i * tile, tile), tile)
@@ -597,11 +655,28 @@
 
             lax.fori_loop(0, width // tile, one, 0)
 
-        for tree in range(2):
-
-            @pl.when(live(tree, t))
-            def _(tree=tree):
-                send(tree, me, trees[tree][0][0], t, (0, 1, 2, 3))
+            @pl.when(in_tree(1, t))
+            def _():
+                send(1, me, trees[1][0][0], t, (0, 1, 2, 3))
+
+        @pl.when(live(0, t))
+        def _():
+            if not doubled:
+                send(0, me, trees[0][0][0], t, (0, 1, 2, 3))
+                return
+
+            def one(i, inner):
+                slot = i // (width // tile)
+                here = i % (width // tile) * tile
+                cols = pl.ds(pl.multiple_of(t * width + here, tile), tile)
+                near_cols = pl.ds(pl.multiple_of((t - low) * width + here, tile), tile)
+                source = me + slot * (peer - me)
+                gathered[rows_of(source), cols] = doubled_step(slot, near_cols)
+                return inner
+
+            lax.fori_loop(0, 2 * (width // tile), one, 0)
+            send(0, me, x, t, (0, 1))
+            send(0, peer, x, t, (0, 1))
 
         for tree in (1, 0):
             relay(t, tree)
@@ -612,6 +687,10 @@
         for tree, (first, second, count) in enumerate(trees)
         if count
     )
+    if doubled:
+        states = extra.at[1, pl.ds(0, 3)]
+        remote(states, states, extra_send, extra_recv.at[0], "fs", peer).wait_recv()
+        extra_copy(3).wait_recv()
     lax.fori_loop(0, chunks + reach, turn, 0)
 
     def finish(k, carry):
@@ -666,10 +745,13 @@
                     ).wait_send()
 
         for number, going_up in zip(moves, (True, False)):
-            drain(number, at, size, going_up, 1)
+            if tree or not doubled:
+                drain(number, at, size, going_up, 1)
         for number, going_up in zip(far_moves, (True, False)):
             drain(number, other, length, going_up, size)
 
+    if doubled:
+        remote(extra.at[0], extra.at[1], extra_send, extra_recv.at[0], "fs", peer).wait_send()
     whole = remote(handed, taken, pair_send, own_recv, "ep", partner)
     whole.wait_send()
     remote(outgoing, arrived, grad_send, own_recv, "ep", partner).wait_send()
@@ -724,6 +806,7 @@
             pltpu.VMEM((rows, columns), jnp.float32),
             pltpu.VMEM((shards, 2, SUBLANES, LANES), jnp.float32),
             pltpu.VMEM((in_bias.shape[0] * rows, TERMS * rows), jnp.bfloat16),
+            pltpu.VMEM((2, 4, rows, max(turned, 1) * (columns // chunks)), jnp.bfloat16),
             pltpu.SemaphoreType.DMA((5,)),
             pltpu.SemaphoreType.DMA((CORES + 1,)),
             pltpu.SemaphoreType.DMA((3,)),
@@ -739,6 +822,8 @@
             pltpu.SemaphoreType.DMA((max(depth, across) - 1, chunks)),
             pltpu.SemaphoreType.DMA((shards, 1 if depth == 2 else max(turned, 1))),
             pltpu.SemaphoreType.DMA((shards, 1 if across == 2 else chunks)),
+            pltpu.SemaphoreType.DMA,
+            pltpu.SemaphoreType.DMA((2,)),
         ],
         compiler_params=pltpu.CompilerParams(
             collective_id=0,

time: 60 us -> 59.4 us (0.990)
  Pallas kernels: 59.2 us -> 58.6 us
where the time goes in v5:
time: 59.4 us; the launch traced here: 59.2 us
  Pallas kernels  58.6 us (99%)
  between operations  0.64 us (1%)
    pallas_call x1, Pallas kernels, per_device(): pl.pallas_call(functools.partial(kernel, groups, depth, across, chunks),...  56.1 us
    pallas_call x1, Pallas kernels, per_device(): pl.pallas_call(flush, out_shape=(jax.ShapeDtypeStruct((1, rows * shards,...  2.46 us

profile of v5, /device:TPU:0, one launch (start us, length us, event | category | flops | bytes accessed | tf_op | source)
XLA Modules:
  0.0 59.2 jit_solution(8217063949367093572)
XLA Ops:
  0.6 56.1 %learned_update.1 = (bf16[128,14336]{1,0:T(8,128)(2,1)S(1)}, f32[16,14336]{1,0:T(8,128)S(1)}, f32[16,14336]{1,0:T(8,128)S(1)}) custom-call(s32[4,4]{1,0:T(4,128)} %counts_hbm.1, f32[6,32]{1,0:T(8,128)} %in_weight_hbm.1, f32[32]{0:T(128)} %in_bias_hbm.1, f32[2,32]{1,0:T(2,128)} %bitcast.1, f32[2]{0:T(128)} %out_bias_hbm.1, ...), custom_call_target="tpu_custom_call" | custom-call | tf_op jit(solution)/shard_map/learned_update/pallas_call | solution.py:785
  56.8 2.5 %flush.1 = (bf16[1,128,14336]{2,1,0:T(8,128)(2,1)}, f32[1,16,14336]{2,1,0:T(8,128)}, f32[1,16,14336]{2,1,0:T(8,128)}) custom-call(bf16[128,14336]{1,0:T(8,128)(2,1)S(1)} %get-tuple-element.6.gathered, f32[16,14336]{1,0:T(8,128)S(1)} %get-tuple-element.7.mom, f32[16,14336]{1,0:T(8,128)S(1)} %get-tuple-element.8.second), custom_call_target="tpu_custom_call" | custom-call | tf_op jit(solution)/shard_map/flush/pallas_call | solution.py:835
